TPU v7x, 32 devices: a whole 2x2x4 slice. The times are simulated.
32 devices in a mesh: dp: 8 (over y, x, core), mp: 4 (over z).
Axes of the slice: x: 2, y: 2, z: 4, core: 2. Of those that a mesh axis runs over, the one named last changes fastest.
Arguments:
- feature_ids: int32 [8, 2048, 8], P('dp'), may hold values from 0 to 4095
- tables: bfloat16 [8, 4096, 128], P('dp'), may hold values from -5 to 5
- table_of_feature: int32 [8], replicated, may hold values from 0 to 7, each once
- cross_down: bfloat16 [2, 1024, 512], P(None, 'mp'), may hold values from -0.1875 to 0.1875
- cross_up: bfloat16 [2, 1024, 512], P(None, 'mp'), may hold values from -0.125 to 0.125
- cross_bias: float32 [2, 1024], P(None, 'mp'), may hold values from -3 to 3
- tower_weight: bfloat16 [1024, 2048], P('dp', 'mp'), may hold values from -0.1875 to 0.1875
- tower_bias: float32 [2048], P('mp'), may hold values from -3 to 3
Outputs:
- hidden: bfloat16 [2048, 2048], P('dp', 'mp')
Inputs may be any that keep to these rules, and one draw needn't show every extreme that they name: `feature_ids`: each id indexes a row of its own table. `table_of_feature`: each table serves exactly one feature.
All inputs are finite; a program needn't handle non-finite values.
Results may differ from a plain program's by a relative error of at most 0.015.
Values may be sent and summed in bfloat16 or wider, within the bound.
No kernel may reach another device: no remote copies, remote signals or barrier semaphores. Data moves between devices by JAX's collectives and lax.ppermute only.
A program may use at most 64 MiB of HBM per device.

v0:
```python
import jax
import jax.numpy as jnp
from jax import lax
from jax.sharding import PartitionSpec as P


def body(
    feature_ids,
    tables,
    table_of_feature,
    cross_down,
    cross_up,
    cross_bias,
    tower_weight,
    tower_bias,
):
    groups = lax.axis_size("dp")
    members = lax.axis_size("mp")
    member = lax.axis_index("mp")
    table_count, batch_size, hot_count = feature_ids.shape
    row_count = batch_size // (groups * members)
    shaped = feature_ids[0].reshape(groups, members, row_count, hot_count)
    own_ids = lax.dynamic_index_in_dim(shaped, member, 1, keepdims=False).reshape(
        groups * row_count, hot_count
    )
    summed = jnp.zeros((groups * row_count, tables.shape[2]), jnp.float32)
    for hot_index in range(hot_count):
        summed = summed + jnp.take(tables[0], own_ids[:, hot_index], axis=0).astype(jnp.float32)
    columns = [summed.astype(jnp.bfloat16)]
    pooled = jnp.stack(columns, axis=1)
    regrouped = lax.all_to_all(pooled, "dp", split_axis=0, concat_axis=1, tiled=True)
    ordered = jnp.take(regrouped, table_of_feature, axis=1)
    by_width = lax.all_to_all(ordered, "mp", split_axis=1, concat_axis=0, tiled=True)
    group_rows = by_width.shape[0]
    embedded = by_width.reshape(group_rows, -1)
    embedded_wide = embedded.astype(jnp.float32)
    crossed = embedded
    layer_total = cross_down.shape[0]
    for layer_index in range(layer_total):
        partial_value = jnp.dot(
            crossed, cross_down[layer_index], preferred_element_type=jnp.float32
        )
        projected = lax.psum(partial_value.astype(jnp.bfloat16), "mp")
        lifted = lax.dot_general(
            projected,
            cross_up[layer_index],
            (((1,), (1,)), ((), ())),
            preferred_element_type=jnp.float32,
        )
        crossed = (
            embedded_wide * (lifted + cross_bias[layer_index]) + crossed.astype(jnp.float32)
        ).astype(jnp.bfloat16)
    full_rows = lax.all_gather(crossed, "mp", axis=1, tiled=True)
    pre_act = jnp.dot(
        full_rows,
        lax.all_gather(tower_weight, "dp", axis=0, tiled=True),
        preferred_element_type=jnp.float32,
    )
    return jax.nn.relu(pre_act + tower_bias).astype(jnp.bfloat16)


def solution(mesh):
    return jax.shard_map(
        body,
        mesh=mesh,
        in_specs=(
            P("dp", None, None),
            P("dp", None, None),
            P(),
            P(None, "mp", None),
            P(None, "mp", None),
            P(None, "mp"),
            P("dp", "mp"),
            P("mp"),
        ),
        out_specs=P("dp", "mp"),
        check_vma=False,
    )
```

profile of v0, /device:TPU:0, one launch (start us, length us, event | category | flops | bytes accessed | tf_op | source)
XLA Modules:
  0.0 143.6 jit_solution(9518459660529289800)
XLA Ops:
  7.4 1.0 reshape_squeeze.3
  8.8 1.3 gather_fusion.2
  10.2 1.3 gather_fusion.3
  11.5 1.3 gather_fusion.4
  12.9 1.3 gather_fusion.5
  14.2 1.3 gather_fusion.6
  15.6 1.3 gather_fusion.7
  17.0 1.3 gather_fusion.8
  18.3 1.3 gather_fusion.1
  19.7 0.8 fusion.16
  21.0 0.7 reduce.4
  21.7 0.7 reshape.125
  22.3 5.3 %all-to-all-start = ((bf16[8,2,4096]{2,1,0:T(2,128)(2,1)}), bf16[8,2,4096]{2,1,0:T(2,128)(2,1)S(1)}, u32[]{:S(2)}, u32[]{:S(2)}) async-start(bf16[8,2,4096]{2,1,0:T(2,128)(2,1)} %reshape.125), calls=%async_computation | async-start | bytes 262144 | tf_op jit(solution)/shard_map/all_to_all | solution.py:31
  27.8 5.4 %all-to-all-done = bf16[8,2,4096]{2,1,0:T(2,128)(2,1)S(1)} async-done(((bf16[8,2,4096]{2,1,0:T(2,128)(2,1)}), bf16[8,2,4096]{2,1,0:T(2,128)(2,1)S(1)}, u32[]{:S(2)}, u32[]{:S(2)}) %all-to-all-start) | async-done | bytes 131104 | tf_op jit(solution)/shard_map/all_to_all | solution.py:31
  34.0 10.6 %all_to_all.33 = bf16[64,8,128]{2,0,1:T(8,128)(2,1)S(1)} all-to-all(bf16[64,8,128]{2,0,1:T(8,128)(2,1)S(1)} %select_bitcast_fusion), channel_id=1, replica_groups=mesh['dp'=8,'mp'=4] {'mp'}, dimensions={1} | all-to-all | bytes 262144 | tf_op jit(solution)/shard_map/all_to_all | solution.py:33
  44.8 0.9 convolution_convert_fusion.1
  45.8 0.6 copy-done.2
  46.4 32.3 %all-reduce.3.cloned.1.call-done = bf16[256,512]{1,0:T(8,128)(2,1)} async-done(((bf16[256,512]{1,0:T(8,128)(2,1)}), bf16[256,512]{1,0:T(8,128)(2,1)}) %all-reduce.3.cloned.1.call-update) | async-done | bytes 262160 | tf_op jit(solution)/shard_map/psum | solution.py:43
  78.8 1.2 fusion.6
  80.0 0.9 convolution_convert_fusion
  81.6 35.0 %all-reduce.5.cloned.1.call-done = bf16[256,512]{1,0:T(8,128)(2,1)} async-done(((bf16[256,512]{1,0:T(8,128)(2,1)}), bf16[256,512]{1,0:T(8,128)(2,1)}) %all-reduce.5.cloned.1.call-update) | async-done | bytes 262160 | tf_op jit(solution)/shard_map/psum | solution.py:43
  116.6 1.2 fusion.7
  117.8 16.0 %all_gather.6 = bf16[256,1024]{1,0:T(8,128)(2,1)S(1)} all-gather(bf16[256,256]{1,0:T(8,128)(2,1)S(1)} %fusion.7), channel_id=1, replica_groups=mesh['dp'=8,'mp'=4] {'mp'}, dimensions={1}, use_global_device_ids=true | all-gather | bytes 655360 | tf_op jit(solution)/shard_map/all_gather | solution.py:53
  133.8 2.4 %fusion.1 = bf16[256,512]{1,0:T(8,128)(2,1)} fusion(bf16[256,1024]{1,0:T(8,128)(2,1)S(1)} %all_gather.6, bf16[1024,512]{1,0:T(8,128)(2,1)} %all-gather.2.cloned.1.call-done, f32[512]{0:T(512)S(1)} %copy-done.4), kind=kOutput, calls=%fused_computation.11 | convolution fusion | flops 268828672 | bytes 1837056 | tf_op jit(solution)/shard_map/dot_general | solution.py:54
  (51 shorter events, 2.5 us)
Async XLA Ops:
  7.4 1.4 %copy-start = (bf16[1,4096,128]{2,1,0:T(8,128)(2,1)S(1)}, bf16[1,4096,128]{2,1,0:T(8,128)(2,1)}, u32[]{:S(2)}) copy-start(bf16[1,4096,128]{2,1,0:T(8,128)(2,1)} %param.11) | copy-start | bytes 3145732
  22.3 5.4 %copy-start.5 = (s32[8]{0:T(128)S(1)}, s32[8]{0:T(128)}, u32[]{:S(2)}) copy-start(s32[8]{0:T(128)} %param.12) | copy-start | bytes 100
  22.3 10.8 %all-to-all-start = ((bf16[8,2,4096]{2,1,0:T(2,128)(2,1)}), bf16[8,2,4096]{2,1,0:T(2,128)(2,1)S(1)}, u32[]{:S(2)}, u32[]{:S(2)}) async-start(bf16[8,2,4096]{2,1,0:T(2,128)(2,1)} %reshape.125), calls=%async_computation | async-start | bytes 262144 | tf_op jit(solution)/shard_map/all_to_all | solution.py:31
  27.7 51.1 %all-reduce.3.cloned.1.call-start = ((), (), s32[]{:S(2)}) async-start(), calls=%async_computation.2 | async-start | bytes 524288 | tf_op jit(solution)/shard_map/psum | solution.py:43
  33.3 11.5 %copy-start.1 = (bf16[2,256,512]{2,1,0:T(8,128)(2,1)S(1)}, bf16[2,256,512]{2,1,0:T(8,128)(2,1)}, u32[]{:S(2)}) copy-start(bf16[2,256,512]{2,1,0:T(8,128)(2,1)} %param.13) | copy-start | bytes 1572868
  44.8 34.0 %copy-start.3 = (bf16[2,256,512]{2,1,0:T(8,128)(2,1)S(1)}, bf16[2,256,512]{2,1,0:T(8,128)(2,1)}, u32[]{:S(2)}) copy-start(bf16[2,256,512]{2,1,0:T(8,128)(2,1)} %param.14) | copy-start | bytes 1572868
  45.8 0.7 copy-start.2
  45.8 70.8 %all-reduce.5.cloned.1.call-start = ((), (), s32[]{:S(2)}) async-start(), calls=%async_computation.3 | async-start | bytes 524288 | tf_op jit(solution)/shard_map/psum | solution.py:43
  81.0 52.8 %all-gather.2.cloned.1.call-start = ((), (), s32[]{:S(2)}) async-start(), calls=%async_computation.4 | async-start | bytes 1179648 | tf_op jit(solution)/shard_map/all_gather | solution.py:56
  117.8 16.0 %copy-start.4 = (f32[512]{0:T(512)S(1)}, f32[512]{0:T(512)}, u32[]{:S(2)}) copy-start(f32[512]{0:T(512)} %param.17) | copy-start | bytes 6148
Sparse Core Ops, SparseCore 0:
  45.9 32.8 all-reduce.2
  81.1 35.4 all-reduce.4
Sparse Core Ops, SparseCore 1:
  83.3 23.1 all-gather.1
where the time goes:
time: 144 us
  waiting for transfers between devices  73.3 us (51%)
  blocking collectives  26.6 us (18%)
  between operations  15.2 us (11%)
  local copies, waits for them, and re-layouts  14.6 us (10%)
  matrix products  6.67 us (5%)
  starting transfers between devices  5.45 us (4%)
  other arithmetic  1.66 us (1%)
    psum x2, waiting for transfers between devices, body(): projected = lax.psum(partial_value.astype(jnp.bfloat16), 'mp')  67.4 us
    all_gather x1, blocking collectives, body(): full_rows = lax.all_gather(crossed, 'mp', axis=1, tiled=True)  16 us
    gather x8, local copies, waits for them, and re-layouts, body(): jnp.take(tables[0], own_ids[:, hot_index], axis=0).astype(jnp.float32)  10.7 us
    all_to_all x1, blocking collectives, body(): lax.all_to_all(ordered, 'mp', split_axis=1, concat_axis=0, tiled=True)  10.6 us
    all_to_all x1, waiting for transfers between devices, body(): lax.all_to_all(pooled, 'dp', split_axis=0, concat_axis=1, tiled=True)  5.4 us
    all_to_all x1, starting transfers between devices, body(): lax.all_to_all(pooled, 'dp', split_axis=0, concat_axis=1, tiled=True)  5.33 us
  transfers between devices with their start and end apart: 4, of which 3 were waited for; matrix products, arithmetic and copies ran while one was open for 1% of the time, Pallas kernels for 0%

commit v1 on v0

--- a/solution.py
+++ b/solution.py
@@ -1,10 +1,23 @@
+import functools
+
 import jax
 import jax.numpy as jnp
 from jax import lax
+from jax.experimental import pallas as pl
+from jax.experimental.pallas import tpu as pltpu
 from jax.sharding import PartitionSpec as P
 
 
-def body(
+GATHER_LIMIT = 12 * 2**20
+
+LANES = 128
+SUBLANES = 16
+
+VMEM = pl.BlockSpec(memory_space=pltpu.VMEM)
+SMEM = pl.BlockSpec(memory_space=pltpu.SMEM)
+
+
+def reduce_body(
     feature_ids,
     tables,
     table_of_feature,
@@ -17,7 +30,7 @@
     groups = lax.axis_size("dp")
     members = lax.axis_size("mp")
     member = lax.axis_index("mp")
-    table_count, batch_size, hot_count = feature_ids.shape
+    _, batch_size, hot_count = feature_ids.shape
     row_count = batch_size // (groups * members)
     shaped = feature_ids[0].reshape(groups, members, row_count, hot_count)
     own_ids = lax.dynamic_index_in_dim(shaped, member, 1, keepdims=False).reshape(
@@ -59,7 +72,280 @@
     return jax.nn.relu(pre_act + tower_bias).astype(jnp.bfloat16)
 
 
+def params(mib):
+    return pltpu.CompilerParams(vmem_limit_bytes=mib * 2**20)
+
+
+def pool_kernel(chunk, place_ref, ids_ref, source_ref, keep_ref, send_ref, table_ref, arrived):
+    vocab, embed = table_ref.shape
+    pieces = arrived.shape[0]
+    size = vocab // pieces
+    copies = [
+        pltpu.make_async_copy(
+            source_ref.at[pl.ds(index * size, size)],
+            table_ref.at[pl.ds(index * size, size)],
+            arrived.at[index],
+        )
+        for index in range(pieces)
+    ]
+    for copy in copies:
+        copy.start()
+    hots, batch = ids_ref.shape
+    chips, rows, _ = keep_ref.shape
+    groups = 2 * chips
+    samples = groups * rows
+    per_group = batch // groups
+    group, member = place_ref[0], place_ref[1]
+    parts = []
+    for owner in range(groups):
+        if rows == LANES // 2:
+            at = pl.multiple_of(owner * per_group + lax.div(member, 2) * LANES, LANES)
+            wide = ids_ref[:, pl.ds(at, LANES)]
+            parts.append(jnp.where(lax.rem(member, 2) == 0, wide[:, :rows], wide[:, rows:]))
+        else:
+            at = pl.multiple_of(owner * per_group + member * rows, LANES)
+            parts.append(ids_ref[:, pl.ds(at, rows)])
+    ids = jnp.concatenate(parts, axis=1)
+    total = jnp.zeros((embed, samples), jnp.float32)
+    row_at = lax.broadcasted_iota(jnp.int16, (chunk, samples), 0)
+    one = jnp.ones((), jnp.bfloat16)
+    zero = jnp.zeros((), jnp.bfloat16)
+    for start in range(0, vocab, chunk):
+        shifted = (ids - start).astype(jnp.int16)
+        counts = None
+        for hot in range(hots):
+            term = jnp.where(shifted[hot : hot + 1, :] == row_at, one, zero)
+            counts = term if counts is None else counts + term
+        if start % size == 0:
+            copies[start // size].wait()
+        total = total + lax.dot_general(
+            table_ref[start : start + chunk, :],
+            counts,
+            (((0,), (0,)), ((), ())),
+            preferred_element_type=jnp.float32,
+        )
+    pooled = total.T.astype(jnp.bfloat16)
+    core = lax.rem(group, 2)
+    half = lax.div(group, 2)
+    for chip in range(chips):
+        at = jnp.bitwise_xor(half, chip)
+        low = pooled[2 * chip * rows : (2 * chip + 1) * rows]
+        high = pooled[(2 * chip + 1) * rows : (2 * chip + 2) * rows]
+        keep_ref[at] = jnp.where(core == 0, low, high)
+        send_ref[at] = jnp.where(core == 0, high, low)
+
+
+def cross_kernel(members, chips, *refs):
+    refs = list(refs)
+
+    def take(count):
+        taken = refs[:count]
+        del refs[:count]
+        return taken
+
+    place_ref, order_ref, down_ref, up_ref, bias_ref, tower_bias_ref = take(6)
+    own_refs, other_refs = take(chips), take(chips)
+    tower_own_refs, tower_other_refs = take(chips), take(chips)
+    piece_refs = take(members)
+    (hidden_ref,) = take(1)
+    embedded_ref, bias_full, down_full, up_full, tower_full = take(5)
+
+    group, member = place_ref[0], place_ref[1]
+    layers, block, _ = down_ref.shape
+    tables = order_ref.shape[0]
+    rows = hidden_ref.shape[0] // members
+    embed = piece_refs[0].shape[1]
+    slice_rows = block // (2 * chips)
+
+    for feature in range(tables):
+        slot = jnp.bitwise_xor(order_ref[feature], group)
+        for step in range(members):
+            embedded_ref[
+                step * rows : (step + 1) * rows, feature * embed : (feature + 1) * embed
+            ] = piece_refs[step][pl.ds(pl.multiple_of(slot * rows, rows), rows), :]
+
+    base = pl.multiple_of(member * block, block)
+    bias_full[:, pl.ds(base, block)] = bias_ref[...]
+    for step in range(1, members):
+        owner = lax.rem(member + members - step, members)
+        for layer in range(layers):
+            for part in range(block // embed):
+                at = tables * rows + (layer * block) // embed + part
+                count = layers * block // embed
+                bias = sum(
+                    piece_refs[step][at + term * count, :].astype(jnp.float32).reshape(1, embed)
+                    for term in range(3)
+                )
+                lane = pl.multiple_of(owner * block + part * embed, embed)
+                bias_full[layer : layer + 1, pl.ds(lane, embed)] = bias
+
+    for chip in range(chips):
+        for core, source in enumerate((tower_own_refs[chip], tower_other_refs[chip])):
+            depth = source.shape[0]
+            slot = jnp.bitwise_xor(group, 2 * chip + core)
+            tower_full[pl.ds(pl.multiple_of(slot * depth, depth), depth), :] = source[...]
+
+    for layer in range(layers):
+        down_full[layer, pl.ds(base, block), :] = down_ref[layer]
+        up_full[layer, pl.ds(base, block), :] = up_ref[layer]
+        first = 2 * layer * slice_rows
+        for step in range(1, members):
+            owner = lax.rem(member + members - step, members)
+            for chip in range(chips):
+                for core, source in enumerate((own_refs[chip], other_refs[chip])):
+                    slot = jnp.bitwise_xor(group, 2 * chip + core)
+                    at = pl.multiple_of(owner * block + slot * slice_rows, slice_rows)
+                    down_full[layer, pl.ds(at, slice_rows), :] = source[
+                        step - 1, first : first + slice_rows
+                    ]
+                    up_full[layer, pl.ds(at, slice_rows), :] = source[
+                        step - 1, first + slice_rows : first + 2 * slice_rows
+                    ]
+
+    embedded = embedded_ref[...]
+    crossed = embedded
+    for layer in range(layers):
+        projected = jnp.dot(
+            crossed, down_full[layer], preferred_element_type=jnp.float32
+        ).astype(jnp.bfloat16)
+        lifted = lax.dot_general(
+            projected,
+            up_full[layer],
+            (((1,), (1,)), ((), ())),
+            preferred_element_type=jnp.float32,
+        )
+        crossed = (
+            embedded.astype(jnp.float32) * (lifted + bias_full[layer : layer + 1, :])
+            + crossed.astype(jnp.float32)
+        ).astype(jnp.bfloat16)
+
+    pre_act = jnp.dot(crossed, tower_full[...], preferred_element_type=jnp.float32)
+    hidden = jnp.maximum(pre_act + tower_bias_ref[...], 0.0).astype(jnp.bfloat16)
+    for step in range(members):
+        owner = lax.rem(member + members - step, members)
+        hidden_ref[pl.ds(pl.multiple_of(owner * rows, rows), rows), :] = hidden[
+            step * rows : (step + 1) * rows
+        ]
+
+
+def shift_over(value, axis, step):
+    count = lax.axis_size(axis)
+    return lax.ppermute(value, axis, [(i, (i + step) % count) for i in range(count)])
+
+
+def flip_over(value, axis, mask):
+    count = lax.axis_size(axis)
+    return lax.ppermute(value, axis, [(i, i ^ mask) for i in range(count)])
+
+
+def split_three(value):
+    high = lax.reduce_precision(value, 8, 7)
+    rest = value - high
+    middle = lax.reduce_precision(rest, 8, 7)
+    return [term.astype(jnp.bfloat16) for term in (high, middle, rest - middle)]
+
+
+def gather_body(
+    feature_ids,
+    tables,
+    table_of_feature,
+    cross_down,
+    cross_up,
+    cross_bias,
+    tower_weight,
+    tower_bias,
+):
+    groups = lax.axis_size("dp")
+    members = lax.axis_size("mp")
+    group = lax.axis_index("dp")
+    member = lax.axis_index("mp")
+    place = jnp.stack([group, member]).astype(jnp.int32)
+    _, batch, _ = feature_ids.shape
+    rows = batch // (groups * members)
+    _, vocab, embed = tables.shape
+    layers, block, rank = cross_down.shape
+    width = block * members
+    slice_rows = block // groups
+    chips = groups // 2
+    steps = range(1, members)
+
+    down_slice = lax.dynamic_slice_in_dim(cross_down, group * slice_rows, slice_rows, 1)
+    up_slice = lax.dynamic_slice_in_dim(cross_up, group * slice_rows, slice_rows, 1)
+    matrices = []
+    for layer in range(layers):
+        matrices += [down_slice[layer], up_slice[layer]]
+    payload = jnp.concatenate(matrices)
+    legs = [shift_over(payload, "mp", step) for step in steps]
+
+    keep, send = pl.pallas_call(
+        functools.partial(pool_kernel, 256),
+        out_shape=[jax.ShapeDtypeStruct((chips, rows, embed), jnp.bfloat16)] * 2,
+        in_specs=[SMEM, VMEM, pl.BlockSpec(memory_space=pl.ANY)],
+        out_specs=[VMEM, VMEM],
+        scratch_shapes=[pltpu.VMEM((vocab, embed), jnp.bfloat16), pltpu.SemaphoreType.DMA((4,))],
+        compiler_params=params(16),
+        cost_estimate=pl.CostEstimate(
+            flops=4 * vocab * groups * rows * embed, bytes_accessed=2**21, transcendentals=0
+        ),
+        name="pool",
+    )(place, feature_ids[0].T, tables[0])
+    crossing = flip_over(send, "dp", 1)
+    both = jnp.stack([keep, crossing], axis=1)
+    held = [both[0]] + [flip_over(both[chip], "dp", 2 * chip) for chip in range(1, chips)]
+    terms = jnp.stack(split_three(cross_bias.reshape(-1))).reshape(-1, embed)
+    bias_rows = -(-terms.shape[0] // SUBLANES) * SUBLANES
+    terms = jnp.pad(terms, ((0, bias_rows - terms.shape[0]), (0, 0)))
+    piece = jnp.concatenate([part.reshape(-1, embed) for part in held] + [terms])
+
+    got = jnp.stack([leg for leg in legs])
+    own = [got] + [flip_over(got, "dp", 2 * chip) for chip in range(1, chips)]
+    other = [flip_over(own[chip], "dp", 1) for chip in range(chips)]
+    pieces = [piece] + [shift_over(piece, "mp", step) for step in steps]
+
+    tower_own = [tower_weight] + [
+        flip_over(tower_weight, "dp", 2 * chip) for chip in range(1, chips)
+    ]
+    tower_other = [flip_over(tower_own[chip], "dp", 1) for chip in range(chips)]
+
+    samples = rows * members
+    units = tower_weight.shape[1]
+    inputs = [place, table_of_feature, cross_down, cross_up, cross_bias]
+    inputs += [tower_bias.reshape(1, units)]
+    inputs += own + other + tower_own + tower_other + pieces
+    return pl.pallas_call(
+        functools.partial(cross_kernel, members, chips),
+        out_shape=jax.ShapeDtypeStruct((samples, units), jnp.bfloat16),
+        in_specs=[SMEM, SMEM] + [VMEM] * (len(inputs) - 2),
+        out_specs=VMEM,
+        scratch_shapes=[
+            pltpu.VMEM((samples, width), jnp.bfloat16),
+            pltpu.VMEM((layers, width), jnp.float32),
+            pltpu.VMEM((layers, width, rank), jnp.bfloat16),
+            pltpu.VMEM((layers, width, rank), jnp.bfloat16),
+            pltpu.VMEM((width, units), jnp.bfloat16),
+        ],
+        compiler_params=params(32),
+        cost_estimate=pl.CostEstimate(
+            flops=2 * samples * width * (2 * layers * rank + units),
+            bytes_accessed=2**23,
+            transcendentals=0,
+        ),
+        name="cross",
+    )(*inputs)
+
+
 def solution(mesh):
+    groups, members = mesh.shape["dp"], mesh.shape["mp"]
+
+    def body(*args):
+        feature_ids, tables, cross_down = args[0], args[1], args[3]
+        _, block, _ = cross_down.shape
+        rows = feature_ids.shape[1] // (groups * members)
+        fits = 4 * cross_down.size * members <= GATHER_LIMIT
+        fits = fits and block % tables.shape[2] == 0 and block % (SUBLANES * groups) == 0
+        fits = fits and (rows == LANES // 2 or rows % LANES == 0) and groups & (groups - 1) == 0
+        return (gather_body if fits else reduce_body)(*args)
+
     return jax.shard_map(
         body,
         mesh=mesh,

time: 144 us -> 59.7 us (0.41)
  waiting for transfers between devices: 73.3 us -> 24.7 us
  blocking collectives: 26.6 us -> 0 us
  starting transfers between devices: 5.45 us -> 24.3 us
  between operations: 15.2 us -> 0.17 us
  local copies, waits for them, and re-layouts: 14.6 us -> 2.14 us
  Pallas kernels: 0 us -> 8 us
  matrix products: 6.67 us -> 0 us
  other arithmetic: 1.66 us -> 0.17 us
    psum x2 -> x0, waiting for transfers between devices: 67.4 us -> none  [body(): projected = lax.psum(partial_value.astype(jnp.bfloat16), 'mp')]
    ppermute x0 -> x24, waiting for transfers between devices: none -> 24.7 us  [the longest x18 16.4 us: flip_over(): return lax.ppermute(value, axis, [(i, i ^ mask) for i in range(count)])]
    ppermute x0 -> x24, starting transfers between devices: none -> 24.3 us  [the longest x6 12.2 us: shift_over(): lax.ppermute(value, axis, [(i, (i + step) % count) for i in range(count)])]
    all_gather x1 -> x0, blocking collectives: 16 us -> none  [body(): full_rows = lax.all_gather(crossed, 'mp', axis=1, tiled=True)]
    gather x9 -> x0, local copies, waits for them, and re-layouts: 11.3 us -> none  [the longest x8 10.7 us: body(): jnp.take(tables[0], own_ids[:, hot_index], axis=0).astype(jnp.float32)]
    all_to_all x1 -> x0, blocking collectives: 10.6 us -> none  [body(): lax.all_to_all(ordered, 'mp', split_axis=1, concat_axis=0, tiled=True)]
    pallas_call x0 -> x2, Pallas kernels: none -> 8 us  [the longest x1 4.74 us: gather_body(): pl.pallas_call(functools.partial(pool_kernel, 256), out_shape=[jax.ShapeD...]
    dot_general x5 -> x0, matrix products: 6.67 us -> none  [the longest x2 2.42 us: body(): lax.dot_general(projected, cross_up[layer_index], (((1,), (1,)), ((), ())...]
  transfers between devices with their start and end apart: 4 -> 24, of which waited for: 3 -> 9; matrix products, arithmetic and copies ran while one was open for 1% -> 0% of each run, Pallas kernels for 0% -> 8%
where the time goes in v1:
time: 59.7 us; the launch traced here: 59.5 us
  waiting for transfers between devices  24.7 us (41%)
  starting transfers between devices  24.3 us (41%)
  Pallas kernels  8 us (13%)
  local copies, waits for them, and re-layouts  2.14 us (4%)
    ppermute x18, waiting for transfers between devices, flip_over(): return lax.ppermute(value, axis, [(i, i ^ mask) for i in range(count)])  16.4 us
    ppermute x6, starting transfers between devices, shift_over(): lax.ppermute(value, axis, [(i, (i + step) % count) for i in range(count)])  12.2 us
    ppermute x18, starting transfers between devices, flip_over(): return lax.ppermute(value, axis, [(i, i ^ mask) for i in range(count)])  12.1 us
    ppermute x6, waiting for transfers between devices, shift_over(): lax.ppermute(value, axis, [(i, (i + step) % count) for i in range(count)])  8.38 us
    pallas_call x1, Pallas kernels, gather_body(): pl.pallas_call(functools.partial(pool_kernel, 256), out_shape=[jax.ShapeD...  4.74 us
    pallas_call x1, Pallas kernels, gather_body(): pl.pallas_call(functools.partial(cross_kernel, members, chips), out_shape...  3.26 us
    unnamed x21, local copies, waits for them, and re-layouts  1.29 us
  transfers between devices with their start and end apart: 24, of which 9 were waited for; matrix products, arithmetic and copies ran while one was open for 0% of the time, Pallas kernels for 8%

profile of v1, /device:TPU:0, one launch (start us, length us, event | category | flops | bytes accessed | tf_op | source)
XLA Modules:
  0.0 59.5 jit_solution(8637359898244632188)
XLA Ops:
  0.0 0.8 %dynamic-slice_bitcast_fusion.2 = (bf16[32,512]{1,0:T(8,128)(2,1)S(1)}, bf16[32,512]{1,0:T(8,128)(2,1)S(1)}, bf16[32,512]{1,0:T(8,128)(2,1)S(1)}, bf16[32,512]{1,0:T(8,128)(2,1)S(1)}) fusion(bf16[2,256,512]{2,1,0:T(8,128)(2,1)} %refs_3_.1, s32[]{:T(128)S(6)} %select_n.4, s32[]{:T(128)S(6)} %add.8, bf16[2,256,512]{2,1,0:T(8,128)(2,1)} %refs_2_.1), kind=kLoop, calls=%fused_computation.17 | loop fusion | bytes 262152 | tf_op jit(solution)/shard_map/squeeze | solution.py:276
  0.9 5.1 %collective-permute-start.2 = (bf16[128,512]{1,0:T(8,128)(2,1)S(1)}, bf16[128,512]{1,0:T(8,128)(2,1)S(1)}, u32[]{:S(2)}, u32[]{:S(2)}) collective-permute-start(bf16[128,512]{1,0:T(8,128)(2,1)S(1)} %pad_maximum_fusion.1), channel_id=1, source_target_pairs={{0,3},{1,0},{2,1},{3,2},{4,7},{5,4},{6,5},{7,6},{8,11},{9,8},{10,9... | collective-permute-start | bytes 393224 | tf_op jit(solution)/shard_map/ppermute | solution.py:233
  6.0 1.0 %collective-permute-start = (bf16[128,512]{1,0:T(8,128)(2,1)S(1)}, bf16[128,512]{1,0:T(8,128)(2,1)S(1)}, u32[]{:S(2)}, u32[]{:S(2)}) collective-permute-start(bf16[128,512]{1,0:T(8,128)(2,1)S(1)} %pad_maximum_fusion.1), channel_id=1, source_target_pairs={{0,1},{1,2},{2,3},{3,0},{4,5},{5,6},{6,7},{7,4},{8,9},{9,10},{10,1... | collective-permute-start | bytes 393224 | tf_op jit(solution)/shard_map/ppermute | solution.py:233
  7.1 1.2 %copy-done.6 = bf16[1,4096,128]{2,1,0:T(8,128)(2,1)S(1)} copy-done((bf16[1,4096,128]{2,1,0:T(8,128)(2,1)S(1)}, bf16[1,4096,128]{2,1,0:T(8,128)(2,1)}, u32[]{:S(2)}) %copy-start.6) | copy-done | bytes 1048600
  8.3 4.7 %pool.1 = (bf16[4,64,128]{2,1,0:T(8,128)(2,1)S(1)}, bf16[4,64,128]{2,1,0:T(8,128)(2,1)S(1)}) custom-call(s32[2]{0:T(128)S(1)} %pad_add_fusion.place_ref.refs_0_, s32[8,2048]{1,0:T(8,128)S(1)} %bitcast.37, bf16[4096,128]{1,0:T(8,128)(2,1)S(1)} %bitcast.36), custom_call_target="tpu_custom_call" | custom-call | flops 1073741824 | bytes 2097152 | tf_op jit(solution)/shard_map/pool/pallas_call | solution.py:280
  13.1 2.5 %collective-permute-start.12 = (bf16[128,512]{1,0:T(8,128)(2,1)S(1)}, bf16[128,512]{1,0:T(8,128)(2,1)S(1)}, u32[]{:S(2)}, u32[]{:S(2)}) collective-permute-start(bf16[128,512]{1,0:T(8,128)(2,1)S(1)} %copy-done.2), channel_id=1, source_target_pairs={{0,24},{4,28},{8,16},{12,20},{16,8},{20,12},{24,0},{28,4},{1,25},{... | collective-permute-start | bytes 393224 | tf_op jit(solution)/shard_map/ppermute | solution.py:238
  15.7 0.6 %collective-permute-start.18 = (bf16[2,64,128]{2,1,0:T(8,128)(2,1)S(1)}, bf16[2,64,128]{2,1,0:T(8,128)(2,1)S(1)}, u32[]{:S(2)}, u32[]{:S(2)}) collective-permute-start(bf16[2,64,128]{2,1,0:T(8,128)(2,1)S(1)} %get-tuple-element.15), channel_id=1, source_target_pairs={{0,8},{4,12},{8,0},{12,4},{16,24},{20,28},{24,16},{28,20},{1,9},{5... | collective-permute-start | bytes 98312 | tf_op jit(solution)/shard_map/ppermute | solution.py:238
  16.4 4.3 %collective-permute-done.18 = bf16[2,64,128]{2,1,0:T(8,128)(2,1)S(1)} collective-permute-done((bf16[2,64,128]{2,1,0:T(8,128)(2,1)S(1)}, bf16[2,64,128]{2,1,0:T(8,128)(2,1)S(1)}, u32[]{:S(2)}, u32[]{:S(2)}) %collective-permute-start.18) | collective-permute-done | bytes 32800 | tf_op jit(solution)/shard_map/ppermute | solution.py:238
  21.2 3.4 %collective-permute-done.19 = bf16[2,64,128]{2,1,0:T(8,128)(2,1)S(1)} collective-permute-done((bf16[2,64,128]{2,1,0:T(8,128)(2,1)S(1)}, bf16[2,64,128]{2,1,0:T(8,128)(2,1)S(1)}, u32[]{:S(2)}, u32[]{:S(2)}) %collective-permute-start.19) | collective-permute-done | bytes 32800 | tf_op jit(solution)/shard_map/ppermute | solution.py:238
  25.1 1.6 %collective-permute-start.10 = (bf16[128,512]{1,0:T(8,128)(2,1)S(1)}, bf16[128,512]{1,0:T(8,128)(2,1)S(1)}, u32[]{:S(2)}, u32[]{:S(2)}) collective-permute-start(bf16[128,512]{1,0:T(8,128)(2,1)S(1)} %copy-done.2), channel_id=1, source_target_pairs={{0,8},{4,12},{8,0},{12,4},{16,24},{20,28},{24,16},{28,20},{1,9},{5... | collective-permute-start | bytes 393224 | tf_op jit(solution)/shard_map/ppermute | solution.py:238
  26.7 1.5 %collective-permute-start.20 = (bf16[2,64,128]{2,1,0:T(8,128)(2,1)S(1)}, bf16[2,64,128]{2,1,0:T(8,128)(2,1)S(1)}, u32[]{:S(2)}, u32[]{:S(2)}) collective-permute-start(bf16[2,64,128]{2,1,0:T(8,128)(2,1)S(1)} %get-tuple-element.13), channel_id=1, source_target_pairs={{0,24},{4,28},{8,16},{12,20},{16,8},{20,12},{24,0},{28,4},{1,25},{... | collective-permute-start | bytes 98312 | tf_op jit(solution)/shard_map/ppermute | solution.py:238
  28.2 1.5 %collective-permute-start.5 = (bf16[3,128,512]{2,1,0:T(8,128)(2,1)S(1)}, bf16[3,128,512]{2,1,0:T(8,128)(2,1)S(1)}, u32[]{:S(2)}, u32[]{:S(2)}) collective-permute-start(bf16[3,128,512]{2,1,0:T(8,128)(2,1)S(1)} %pad_maximum_fusion.refs_6_), channel_id=1, source_target_pairs={{0,24},{4,28},{8,16},{12,20},{16,8},{20,12},{24,0},{28,4},{1,25},{... | collective-permute-start | bytes 1179656 | tf_op jit(solution)/shard_map/ppermute | solution.py:238
  29.7 3.5 %collective-permute-done.20 = bf16[2,64,128]{2,1,0:T(8,128)(2,1)S(1)} collective-permute-done((bf16[2,64,128]{2,1,0:T(8,128)(2,1)S(1)}, bf16[2,64,128]{2,1,0:T(8,128)(2,1)S(1)}, u32[]{:S(2)}, u32[]{:S(2)}) %collective-permute-start.20) | collective-permute-done | bytes 32800 | tf_op jit(solution)/shard_map/ppermute | solution.py:238
  33.2 0.5 collective-permute-start.4
  33.7 1.5 %collective-permute-start.3 = (bf16[3,128,512]{2,1,0:T(8,128)(2,1)S(1)}, bf16[3,128,512]{2,1,0:T(8,128)(2,1)S(1)}, u32[]{:S(2)}, u32[]{:S(2)}) collective-permute-start(bf16[3,128,512]{2,1,0:T(8,128)(2,1)S(1)} %pad_maximum_fusion.refs_6_), channel_id=1, source_target_pairs={{0,8},{4,12},{8,0},{12,4},{16,24},{20,28},{24,16},{28,20},{1,9},{5... | collective-permute-start | bytes 1179656 | tf_op jit(solution)/shard_map/ppermute | solution.py:238
  35.3 2.9 %collective-permute-start.23 = (bf16[528,128]{1,0:T(8,128)(2,1)S(1)}, bf16[528,128]{1,0:T(8,128)(2,1)S(1)}, u32[]{:S(2)}, u32[]{:S(2)}) collective-permute-start(bf16[528,128]{1,0:T(8,128)(2,1)S(1)} %constant_dynamic-update-slice_fusion.refs_22_), channel_id=1, source_target_pairs={{0,3},{1,0},{2,1},{3,2},{4,7},{5,4},{6,5},{7,6},{8,11},{9,8},{10,9... | collective-permute-start | bytes 405512 | tf_op jit(solution)/shard_map/ppermute | solution.py:233
  38.1 1.3 %collective-permute-done.13.refs_18_ = bf16[128,512]{1,0:T(8,128)(2,1)S(1)} collective-permute-done((bf16[128,512]{1,0:T(8,128)(2,1)S(1)}, bf16[128,512]{1,0:T(8,128)(2,1)S(1)}, u32[]{:S(2)}, u32[]{:S(2)}) %collective-permute-start.13) | collective-permute-done | bytes 131104 | tf_op jit(solution)/shard_map/ppermute | solution.py:238
  39.5 1.1 %collective-permute-start.22 = (bf16[528,128]{1,0:T(8,128)(2,1)S(1)}, bf16[528,128]{1,0:T(8,128)(2,1)S(1)}, u32[]{:S(2)}, u32[]{:S(2)}) collective-permute-start(bf16[528,128]{1,0:T(8,128)(2,1)S(1)} %constant_dynamic-update-slice_fusion.refs_22_), channel_id=1, source_target_pairs={{0,2},{1,3},{2,0},{3,1},{4,6},{5,7},{6,4},{7,5},{8,10},{9,11},{10,... | collective-permute-start | bytes 405512 | tf_op jit(solution)/shard_map/ppermute | solution.py:233
  40.8 2.0 %collective-permute-start.21 = (bf16[528,128]{1,0:T(8,128)(2,1)S(1)}, bf16[528,128]{1,0:T(8,128)(2,1)S(1)}, u32[]{:S(2)}, u32[]{:S(2)}) collective-permute-start(bf16[528,128]{1,0:T(8,128)(2,1)S(1)} %constant_dynamic-update-slice_fusion.refs_22_), channel_id=1, source_target_pairs={{0,1},{1,2},{2,3},{3,0},{4,5},{5,6},{6,7},{7,4},{8,9},{9,10},{10,1... | collective-permute-start | bytes 405512 | tf_op jit(solution)/shard_map/ppermute | solution.py:233
  42.8 8.2 %collective-permute-done.22.refs_24_ = bf16[528,128]{1,0:T(8,128)(2,1)S(1)} collective-permute-done((bf16[528,128]{1,0:T(8,128)(2,1)S(1)}, bf16[528,128]{1,0:T(8,128)(2,1)S(1)}, u32[]{:S(2)}, u32[]{:S(2)}) %collective-permute-start.22) | collective-permute-done | bytes 135200 | tf_op jit(solution)/shard_map/ppermute | solution.py:233
  52.1 0.8 %collective-permute-done.16.refs_21_ = bf16[128,512]{1,0:T(8,128)(2,1)S(1)} collective-permute-done((bf16[128,512]{1,0:T(8,128)(2,1)S(1)}, bf16[128,512]{1,0:T(8,128)(2,1)S(1)}, u32[]{:S(2)}, u32[]{:S(2)}) %collective-permute-start.16) | collective-permute-done | bytes 131104 | tf_op jit(solution)/shard_map/ppermute | solution.py:238
  53.1 1.7 %collective-permute-done.15.refs_20_ = bf16[128,512]{1,0:T(8,128)(2,1)S(1)} collective-permute-done((bf16[128,512]{1,0:T(8,128)(2,1)S(1)}, bf16[128,512]{1,0:T(8,128)(2,1)S(1)}, u32[]{:S(2)}, u32[]{:S(2)}) %collective-permute-start.15) | collective-permute-done | bytes 131104 | tf_op jit(solution)/shard_map/ppermute | solution.py:238
  54.9 1.2 %collective-permute-done.14.refs_19_ = bf16[128,512]{1,0:T(8,128)(2,1)S(1)} collective-permute-done((bf16[128,512]{1,0:T(8,128)(2,1)S(1)}, bf16[128,512]{1,0:T(8,128)(2,1)S(1)}, u32[]{:S(2)}, u32[]{:S(2)}) %collective-permute-start.14) | collective-permute-done | bytes 131104 | tf_op jit(solution)/shard_map/ppermute | solution.py:238
  56.2 3.3 %cross.1 = bf16[256,512]{1,0:T(8,128)(2,1)} custom-call(s32[2]{0:T(128)S(1)} %pad_add_fusion.place_ref.refs_0_, s32[8]{0:T(128)S(1)} %copy-done.5, bf16[2,256,512]{2,1,0:T(8,128)(2,1)S(1)} %copy-done, bf16[2,256,512]{2,1,0:T(8,128)(2,1)S(1)} %copy-done.1, f32[2,256]{1,0:T(2,128)S(1)} %copy-done.3, f32[1,512]{1,0:T(1,128)S(1)} %bitcast.35, ...), custom_call_target="tpu_custom_call" | custom-call | flops 1342177280 | bytes 8388608 | tf_op jit(solution)/shard_map/cross/pallas_call | solution.py:315
  (56 shorter events, 2.9 us)
Async XLA Ops:
  0.9 24.3 %collective-permute-start.2 = (bf16[128,512]{1,0:T(8,128)(2,1)S(1)}, bf16[128,512]{1,0:T(8,128)(2,1)S(1)}, u32[]{:S(2)}, u32[]{:S(2)}) collective-permute-start(bf16[128,512]{1,0:T(8,128)(2,1)S(1)} %pad_maximum_fusion.1), channel_id=1, source_target_pairs={{0,3},{1,0},{2,1},{3,2},{4,7},{5,4},{6,5},{7,6},{8,11},{9,8},{10,9... | collective-permute-start | bytes 393224 | tf_op jit(solution)/shard_map/ppermute | solution.py:233
  6.0 20.7 %collective-permute-start.1 = (bf16[128,512]{1,0:T(8,128)(2,1)S(1)}, bf16[128,512]{1,0:T(8,128)(2,1)S(1)}, u32[]{:S(2)}, u32[]{:S(2)}) collective-permute-start(bf16[128,512]{1,0:T(8,128)(2,1)S(1)} %pad_maximum_fusion.1), channel_id=1, source_target_pairs={{0,2},{1,3},{2,0},{3,1},{4,6},{5,7},{6,4},{7,5},{8,10},{9,11},{10,... | collective-permute-start | bytes 393224 | tf_op jit(solution)/shard_map/ppermute | solution.py:233
  6.0 22.2 %collective-permute-start = (bf16[128,512]{1,0:T(8,128)(2,1)S(1)}, bf16[128,512]{1,0:T(8,128)(2,1)S(1)}, u32[]{:S(2)}, u32[]{:S(2)}) collective-permute-start(bf16[128,512]{1,0:T(8,128)(2,1)S(1)} %pad_maximum_fusion.1), channel_id=1, source_target_pairs={{0,1},{1,2},{2,3},{3,0},{4,5},{5,6},{6,7},{7,4},{8,9},{9,10},{10,1... | collective-permute-start | bytes 393224 | tf_op jit(solution)/shard_map/ppermute | solution.py:233
  13.1 2.7 %collective-permute-start.17 = (bf16[4,64,128]{2,1,0:T(8,128)(2,1)S(1)}, bf16[4,64,128]{2,1,0:T(8,128)(2,1)S(1)}, u32[]{:S(2)}, u32[]{:S(2)}) collective-permute-start(bf16[4,64,128]{2,1,0:T(8,128)(2,1)S(1)} %get-tuple-element.8), channel_id=1, source_target_pairs={{0,4},{4,0},{8,12},{12,8},{16,20},{20,16},{24,28},{28,24},{1,5},{5... | collective-permute-start | bytes 196616 | tf_op jit(solution)/shard_map/ppermute | solution.py:238
  13.1 20.6 %collective-permute-start.12 = (bf16[128,512]{1,0:T(8,128)(2,1)S(1)}, bf16[128,512]{1,0:T(8,128)(2,1)S(1)}, u32[]{:S(2)}, u32[]{:S(2)}) collective-permute-start(bf16[128,512]{1,0:T(8,128)(2,1)S(1)} %copy-done.2), channel_id=1, source_target_pairs={{0,24},{4,28},{8,16},{12,20},{16,8},{20,12},{24,0},{28,4},{1,25},{... | collective-permute-start | bytes 393224 | tf_op jit(solution)/shard_map/ppermute | solution.py:238
  15.7 5.0 %collective-permute-start.18 = (bf16[2,64,128]{2,1,0:T(8,128)(2,1)S(1)}, bf16[2,64,128]{2,1,0:T(8,128)(2,1)S(1)}, u32[]{:S(2)}, u32[]{:S(2)}) collective-permute-start(bf16[2,64,128]{2,1,0:T(8,128)(2,1)S(1)} %get-tuple-element.15), channel_id=1, source_target_pairs={{0,8},{4,12},{8,0},{12,4},{16,24},{20,28},{24,16},{28,20},{1,9},{5... | collective-permute-start | bytes 98312 | tf_op jit(solution)/shard_map/ppermute | solution.py:238
  20.7 3.9 %collective-permute-start.19 = (bf16[2,64,128]{2,1,0:T(8,128)(2,1)S(1)}, bf16[2,64,128]{2,1,0:T(8,128)(2,1)S(1)}, u32[]{:S(2)}, u32[]{:S(2)}) collective-permute-start(bf16[2,64,128]{2,1,0:T(8,128)(2,1)S(1)} %get-tuple-element.16), channel_id=1, source_target_pairs={{0,16},{4,20},{8,24},{12,28},{16,0},{20,4},{24,8},{28,12},{1,17},{... | collective-permute-start | bytes 98312 | tf_op jit(solution)/shard_map/ppermute | solution.py:238
  24.6 10.7 %collective-permute-start.11 = (bf16[128,512]{1,0:T(8,128)(2,1)S(1)}, bf16[128,512]{1,0:T(8,128)(2,1)S(1)}, u32[]{:S(2)}, u32[]{:S(2)}) collective-permute-start(bf16[128,512]{1,0:T(8,128)(2,1)S(1)} %copy-done.2), channel_id=1, source_target_pairs={{0,16},{4,20},{8,24},{12,28},{16,0},{20,4},{24,8},{28,12},{1,17},{... | collective-permute-start | bytes 393224 | tf_op jit(solution)/shard_map/ppermute | solution.py:238
  25.1 13.0 %collective-permute-start.10 = (bf16[128,512]{1,0:T(8,128)(2,1)S(1)}, bf16[128,512]{1,0:T(8,128)(2,1)S(1)}, u32[]{:S(2)}, u32[]{:S(2)}) collective-permute-start(bf16[128,512]{1,0:T(8,128)(2,1)S(1)} %copy-done.2), channel_id=1, source_target_pairs={{0,8},{4,12},{8,0},{12,4},{16,24},{20,28},{24,16},{28,20},{1,9},{5... | collective-permute-start | bytes 393224 | tf_op jit(solution)/shard_map/ppermute | solution.py:238
  26.7 6.5 %collective-permute-start.20 = (bf16[2,64,128]{2,1,0:T(8,128)(2,1)S(1)}, bf16[2,64,128]{2,1,0:T(8,128)(2,1)S(1)}, u32[]{:S(2)}, u32[]{:S(2)}) collective-permute-start(bf16[2,64,128]{2,1,0:T(8,128)(2,1)S(1)} %get-tuple-element.13), channel_id=1, source_target_pairs={{0,24},{4,28},{8,16},{12,20},{16,8},{20,12},{24,0},{28,4},{1,25},{... | collective-permute-start | bytes 98312 | tf_op jit(solution)/shard_map/ppermute | solution.py:238
  28.2 23.3 %collective-permute-start.5 = (bf16[3,128,512]{2,1,0:T(8,128)(2,1)S(1)}, bf16[3,128,512]{2,1,0:T(8,128)(2,1)S(1)}, u32[]{:S(2)}, u32[]{:S(2)}) collective-permute-start(bf16[3,128,512]{2,1,0:T(8,128)(2,1)S(1)} %pad_maximum_fusion.refs_6_), channel_id=1, source_target_pairs={{0,24},{4,28},{8,16},{12,20},{16,8},{20,12},{24,0},{28,4},{1,25},{... | collective-permute-start | bytes 1179656 | tf_op jit(solution)/shard_map/ppermute | solution.py:238
  33.2 18.4 %collective-permute-start.4 = (bf16[3,128,512]{2,1,0:T(8,128)(2,1)S(1)}, bf16[3,128,512]{2,1,0:T(8,128)(2,1)S(1)}, u32[]{:S(2)}, u32[]{:S(2)}) collective-permute-start(bf16[3,128,512]{2,1,0:T(8,128)(2,1)S(1)} %pad_maximum_fusion.refs_6_), channel_id=1, source_target_pairs={{0,16},{4,20},{8,24},{12,28},{16,0},{20,4},{24,8},{28,12},{1,17},{... | collective-permute-start | bytes 1179656 | tf_op jit(solution)/shard_map/ppermute | solution.py:238
  33.7 18.3 %collective-permute-start.3 = (bf16[3,128,512]{2,1,0:T(8,128)(2,1)S(1)}, bf16[3,128,512]{2,1,0:T(8,128)(2,1)S(1)}, u32[]{:S(2)}, u32[]{:S(2)}) collective-permute-start(bf16[3,128,512]{2,1,0:T(8,128)(2,1)S(1)} %pad_maximum_fusion.refs_6_), channel_id=1, source_target_pairs={{0,8},{4,12},{8,0},{12,4},{16,24},{20,28},{24,16},{28,20},{1,9},{5... | collective-permute-start | bytes 1179656 | tf_op jit(solution)/shard_map/ppermute | solution.py:238
  35.3 5.5 %collective-permute-start.23 = (bf16[528,128]{1,0:T(8,128)(2,1)S(1)}, bf16[528,128]{1,0:T(8,128)(2,1)S(1)}, u32[]{:S(2)}, u32[]{:S(2)}) collective-permute-start(bf16[528,128]{1,0:T(8,128)(2,1)S(1)} %constant_dynamic-update-slice_fusion.refs_22_), channel_id=1, source_target_pairs={{0,3},{1,0},{2,1},{3,2},{4,7},{5,4},{6,5},{7,6},{8,11},{9,8},{10,9... | collective-permute-start | bytes 405512 | tf_op jit(solution)/shard_map/ppermute | solution.py:233
  38.1 1.3 %collective-permute-start.13 = (bf16[128,512]{1,0:T(8,128)(2,1)S(1)}, bf16[128,512]{1,0:T(8,128)(2,1)S(1)}, u32[]{:S(2)}, u32[]{:S(2)}) collective-permute-start(bf16[128,512]{1,0:T(8,128)(2,1)S(1)} %copy-done.2), channel_id=1, source_target_pairs={{0,4},{4,0},{8,12},{12,8},{16,20},{20,16},{24,28},{28,24},{1,5},{5... | collective-permute-start | bytes 393224 | tf_op jit(solution)/shard_map/ppermute | solution.py:238
  39.5 11.5 %collective-permute-start.22 = (bf16[528,128]{1,0:T(8,128)(2,1)S(1)}, bf16[528,128]{1,0:T(8,128)(2,1)S(1)}, u32[]{:S(2)}, u32[]{:S(2)}) collective-permute-start(bf16[528,128]{1,0:T(8,128)(2,1)S(1)} %constant_dynamic-update-slice_fusion.refs_22_), channel_id=1, source_target_pairs={{0,2},{1,3},{2,0},{3,1},{4,6},{5,7},{6,4},{7,5},{8,10},{9,11},{10,... | collective-permute-start | bytes 405512 | tf_op jit(solution)/shard_map/ppermute | solution.py:233
  40.8 10.3 %collective-permute-start.21 = (bf16[528,128]{1,0:T(8,128)(2,1)S(1)}, bf16[528,128]{1,0:T(8,128)(2,1)S(1)}, u32[]{:S(2)}, u32[]{:S(2)}) collective-permute-start(bf16[528,128]{1,0:T(8,128)(2,1)S(1)} %constant_dynamic-update-slice_fusion.refs_22_), channel_id=1, source_target_pairs={{0,1},{1,2},{2,3},{3,0},{4,5},{5,6},{6,7},{7,4},{8,9},{9,10},{10,1... | collective-permute-start | bytes 405512 | tf_op jit(solution)/shard_map/ppermute | solution.py:233
  51.0 5.1 %collective-permute-start.6 = (bf16[3,128,512]{2,1,0:T(8,128)(2,1)S(1)}, bf16[3,128,512]{2,1,0:T(8,128)(2,1)S(1)}, u32[]{:S(2)}, u32[]{:S(2)}) collective-permute-start(bf16[3,128,512]{2,1,0:T(8,128)(2,1)S(1)} %pad_maximum_fusion.refs_6_), channel_id=1, source_target_pairs={{0,4},{4,0},{8,12},{12,8},{16,20},{20,16},{24,28},{28,24},{1,5},{5... | collective-permute-start | bytes 1179656 | tf_op jit(solution)/shard_map/ppermute | solution.py:238
  51.1 1.9 %collective-permute-start.16 = (bf16[128,512]{1,0:T(8,128)(2,1)S(1)}, bf16[128,512]{1,0:T(8,128)(2,1)S(1)}, u32[]{:S(2)}, u32[]{:S(2)}) collective-permute-start(bf16[128,512]{1,0:T(8,128)(2,1)S(1)} %collective-permute-done.12.refs_17_), channel_id=1, source_target_pairs={{0,4},{4,0},{8,12},{12,8},{16,20},{20,16},{24,28},{28,24},{1,5},{5... | collective-permute-start | bytes 393224 | tf_op jit(solution)/shard_map/ppermute | solution.py:238
  51.5 4.6 %collective-permute-start.9 = (bf16[3,128,512]{2,1,0:T(8,128)(2,1)S(1)}, bf16[3,128,512]{2,1,0:T(8,128)(2,1)S(1)}, u32[]{:S(2)}, u32[]{:S(2)}) collective-permute-start(bf16[3,128,512]{2,1,0:T(8,128)(2,1)S(1)} %collective-permute-done.5.refs_9_), channel_id=1, source_target_pairs={{0,4},{4,0},{8,12},{12,8},{16,20},{20,16},{24,28},{28,24},{1,5},{5... | collective-permute-start | bytes 1179656 | tf_op jit(solution)/shard_map/ppermute | solution.py:238
  51.6 4.6 %collective-permute-start.8 = (bf16[3,128,512]{2,1,0:T(8,128)(2,1)S(1)}, bf16[3,128,512]{2,1,0:T(8,128)(2,1)S(1)}, u32[]{:S(2)}, u32[]{:S(2)}) collective-permute-start(bf16[3,128,512]{2,1,0:T(8,128)(2,1)S(1)} %collective-permute-done.4.refs_8_), channel_id=1, source_target_pairs={{0,4},{4,0},{8,12},{12,8},{16,20},{20,16},{24,28},{28,24},{1,5},{5... | collective-permute-start | bytes 1179656 | tf_op jit(solution)/shard_map/ppermute | solution.py:238
  52.0 4.1 %collective-permute-start.7 = (bf16[3,128,512]{2,1,0:T(8,128)(2,1)S(1)}, bf16[3,128,512]{2,1,0:T(8,128)(2,1)S(1)}, u32[]{:S(2)}, u32[]{:S(2)}) collective-permute-start(bf16[3,128,512]{2,1,0:T(8,128)(2,1)S(1)} %collective-permute-done.3.refs_7_), channel_id=1, source_target_pairs={{0,4},{4,0},{8,12},{12,8},{16,20},{20,16},{24,28},{28,24},{1,5},{5... | collective-permute-start | bytes 1179656 | tf_op jit(solution)/shard_map/ppermute | solution.py:238
  52.9 1.9 %collective-permute-start.15 = (bf16[128,512]{1,0:T(8,128)(2,1)S(1)}, bf16[128,512]{1,0:T(8,128)(2,1)S(1)}, u32[]{:S(2)}, u32[]{:S(2)}) collective-permute-start(bf16[128,512]{1,0:T(8,128)(2,1)S(1)} %collective-permute-done.11.refs_16_), channel_id=1, source_target_pairs={{0,4},{4,0},{8,12},{12,8},{16,20},{20,16},{24,28},{28,24},{1,5},{5... | collective-permute-start | bytes 393224 | tf_op jit(solution)/shard_map/ppermute | solution.py:238
  54.8 1.3 %collective-permute-start.14 = (bf16[128,512]{1,0:T(8,128)(2,1)S(1)}, bf16[128,512]{1,0:T(8,128)(2,1)S(1)}, u32[]{:S(2)}, u32[]{:S(2)}) collective-permute-start(bf16[128,512]{1,0:T(8,128)(2,1)S(1)} %collective-permute-done.10.refs_15_), channel_id=1, source_target_pairs={{0,4},{4,0},{8,12},{12,8},{16,20},{20,16},{24,28},{28,24},{1,5},{5... | collective-permute-start | bytes 393224 | tf_op jit(solution)/shard_map/ppermute | solution.py:238
  (8 other events, 136.5 us)

commit v2 on v1

--- a/solution.py
+++ b/solution.py
@@ -12,6 +12,7 @@
 
 LANES = 128
 SUBLANES = 16
+PLANE = 4
 
 VMEM = pl.BlockSpec(memory_space=pltpu.VMEM)
 SMEM = pl.BlockSpec(memory_space=pltpu.SMEM)
@@ -76,36 +77,38 @@
     return pltpu.CompilerParams(vmem_limit_bytes=mib * 2**20)
 
 
-def pool_kernel(chunk, place_ref, ids_ref, source_ref, keep_ref, send_ref, table_ref, arrived):
+def pool_kernel(
+    chunk, ids_ref, bias_ref, table_ref, keep_ref, send_ref, terms_ref
+):
     vocab, embed = table_ref.shape
-    pieces = arrived.shape[0]
-    size = vocab // pieces
-    copies = [
-        pltpu.make_async_copy(
-            source_ref.at[pl.ds(index * size, size)],
-            table_ref.at[pl.ds(index * size, size)],
-            arrived.at[index],
-        )
-        for index in range(pieces)
-    ]
-    for copy in copies:
-        copy.start()
+    rest = bias_ref[...]
+    layers, block = rest.shape
+    parts = block // embed
+    terms_ref[...] = jnp.zeros_like(terms_ref)
+    for term in range(3):
+        rounded = rest.astype(jnp.bfloat16)
+        for layer in range(layers):
+            for part in range(parts):
+                terms_ref[pl.ds((term * layers + layer) * parts + part, 1), :] = rounded[
+                    layer : layer + 1, part * embed : (part + 1) * embed
+                ]
+        rest = rest - rounded.astype(jnp.float32)
     hots, batch = ids_ref.shape
     chips, rows, _ = keep_ref.shape
     groups = 2 * chips
     samples = groups * rows
     per_group = batch // groups
-    group, member = place_ref[0], place_ref[1]
-    parts = []
+    group, member = lax.axis_index("dp"), lax.axis_index("mp")
+    wanted = []
     for owner in range(groups):
         if rows == LANES // 2:
             at = pl.multiple_of(owner * per_group + lax.div(member, 2) * LANES, LANES)
             wide = ids_ref[:, pl.ds(at, LANES)]
-            parts.append(jnp.where(lax.rem(member, 2) == 0, wide[:, :rows], wide[:, rows:]))
+            wanted.append(jnp.where(lax.rem(member, 2) == 0, wide[:, :rows], wide[:, rows:]))
         else:
             at = pl.multiple_of(owner * per_group + member * rows, LANES)
-            parts.append(ids_ref[:, pl.ds(at, rows)])
-    ids = jnp.concatenate(parts, axis=1)
+            wanted.append(ids_ref[:, pl.ds(at, rows)])
+    ids = jnp.concatenate(wanted, axis=1)
     total = jnp.zeros((embed, samples), jnp.float32)
     row_at = lax.broadcasted_iota(jnp.int16, (chunk, samples), 0)
     one = jnp.ones((), jnp.bfloat16)
@@ -116,8 +119,6 @@
         for hot in range(hots):
             term = jnp.where(shifted[hot : hot + 1, :] == row_at, one, zero)
             counts = term if counts is None else counts + term
-        if start % size == 0:
-            copies[start // size].wait()
         total = total + lax.dot_general(
             table_ref[start : start + chunk, :],
             counts,
@@ -143,14 +144,14 @@
         del refs[:count]
         return taken
 
-    place_ref, order_ref, down_ref, up_ref, bias_ref, tower_bias_ref = take(6)
+    order_ref, down_ref, up_ref, tower_bias_ref = take(4)
     own_refs, other_refs = take(chips), take(chips)
     tower_own_refs, tower_other_refs = take(chips), take(chips)
     piece_refs = take(members)
     (hidden_ref,) = take(1)
     embedded_ref, bias_full, down_full, up_full, tower_full = take(5)
 
-    group, member = place_ref[0], place_ref[1]
+    group, member = lax.axis_index("dp"), lax.axis_index("mp")
     layers, block, _ = down_ref.shape
     tables = order_ref.shape[0]
     rows = hidden_ref.shape[0] // members
@@ -165,9 +166,8 @@
             ] = piece_refs[step][pl.ds(pl.multiple_of(slot * rows, rows), rows), :]
 
     base = pl.multiple_of(member * block, block)
-    bias_full[:, pl.ds(base, block)] = bias_ref[...]
-    for step in range(1, members):
-        owner = lax.rem(member + members - step, members)
+    for step in range(members):
+        owner = jnp.bitwise_xor(member, step)
         for layer in range(layers):
             for part in range(block // embed):
                 at = tables * rows + (layer * block) // embed + part
@@ -179,10 +179,15 @@
                 lane = pl.multiple_of(owner * block + part * embed, embed)
                 bias_full[layer : layer + 1, pl.ds(lane, embed)] = bias
 
+    core = lax.rem(group, 2)
+    near, far = 2 + 2 * core, 4 - 2 * core
+    own_slots = [jnp.bitwise_xor(group, mask) for mask in (0, near, far, 6)]
+    other_slots = [jnp.bitwise_xor(group, mask) for mask in (1, far + 1, near + 1, 7)]
+
     for chip in range(chips):
-        for core, source in enumerate((tower_own_refs[chip], tower_other_refs[chip])):
+        for side, source in enumerate((tower_own_refs[chip], tower_other_refs[chip])):
+            slot = jnp.bitwise_xor(group, 2 * chip + side)
             depth = source.shape[0]
-            slot = jnp.bitwise_xor(group, 2 * chip + core)
             tower_full[pl.ds(pl.multiple_of(slot * depth, depth), depth), :] = source[...]
 
     for layer in range(layers):
@@ -190,10 +195,10 @@
         up_full[layer, pl.ds(base, block), :] = up_ref[layer]
         first = 2 * layer * slice_rows
         for step in range(1, members):
-            owner = lax.rem(member + members - step, members)
+            owner = jnp.bitwise_xor(member, step)
             for chip in range(chips):
-                for core, source in enumerate((own_refs[chip], other_refs[chip])):
-                    slot = jnp.bitwise_xor(group, 2 * chip + core)
+                for slots, sources in ((own_slots, own_refs), (other_slots, other_refs)):
+                    source, slot = sources[chip], slots[chip]
                     at = pl.multiple_of(owner * block + slot * slice_rows, slice_rows)
                     down_full[layer, pl.ds(at, slice_rows), :] = source[
                         step - 1, first : first + slice_rows
@@ -222,27 +227,28 @@
     pre_act = jnp.dot(crossed, tower_full[...], preferred_element_type=jnp.float32)
     hidden = jnp.maximum(pre_act + tower_bias_ref[...], 0.0).astype(jnp.bfloat16)
     for step in range(members):
-        owner = lax.rem(member + members - step, members)
+        owner = jnp.bitwise_xor(member, step)
         hidden_ref[pl.ds(pl.multiple_of(owner * rows, rows), rows), :] = hidden[
             step * rows : (step + 1) * rows
         ]
 
 
-def shift_over(value, axis, step):
-    count = lax.axis_size(axis)
-    return lax.ppermute(value, axis, [(i, (i + step) % count) for i in range(count)])
-
-
 def flip_over(value, axis, mask):
     count = lax.axis_size(axis)
     return lax.ppermute(value, axis, [(i, i ^ mask) for i in range(count)])
 
 
-def split_three(value):
-    high = lax.reduce_precision(value, 8, 7)
-    rest = value - high
-    middle = lax.reduce_precision(rest, 8, 7)
-    return [term.astype(jnp.bfloat16) for term in (high, middle, rest - middle)]
+def by_role(value, axis, even_mask, odd_mask):
+    count = lax.axis_size(axis)
+    pairs = [(i, i ^ (even_mask if i % 2 == 0 else odd_mask)) for i in range(count)]
+    return lax.ppermute(value, axis, pairs)
+
+
+def spread(value):
+    near = by_role(value, "dp", 2, 4)
+    far = by_role(value, "dp", 4, 2)
+    across = by_role(near, "dp", 4, 2)
+    return [value, near, far, across]
 
 
 def gather_body(
@@ -258,8 +264,6 @@
     groups = lax.axis_size("dp")
     members = lax.axis_size("mp")
     group = lax.axis_index("dp")
-    member = lax.axis_index("mp")
-    place = jnp.stack([group, member]).astype(jnp.int32)
     _, batch, _ = feature_ids.shape
     rows = batch // (groups * members)
     _, vocab, embed = tables.shape
@@ -275,32 +279,31 @@
     for layer in range(layers):
         matrices += [down_slice[layer], up_slice[layer]]
     payload = jnp.concatenate(matrices)
-    legs = [shift_over(payload, "mp", step) for step in steps]
-
-    keep, send = pl.pallas_call(
+    legs = [flip_over(payload, "mp", step) for step in steps]
+
+    bias_rows = -(-3 * cross_bias.size // embed // SUBLANES) * SUBLANES
+
+    keep, send, terms = pl.pallas_call(
         functools.partial(pool_kernel, 256),
-        out_shape=[jax.ShapeDtypeStruct((chips, rows, embed), jnp.bfloat16)] * 2,
-        in_specs=[SMEM, VMEM, pl.BlockSpec(memory_space=pl.ANY)],
-        out_specs=[VMEM, VMEM],
-        scratch_shapes=[pltpu.VMEM((vocab, embed), jnp.bfloat16), pltpu.SemaphoreType.DMA((4,))],
+        out_shape=[jax.ShapeDtypeStruct((chips, rows, embed), jnp.bfloat16)] * 2
+        + [jax.ShapeDtypeStruct((bias_rows, embed), jnp.bfloat16)],
+        in_specs=[VMEM, VMEM, VMEM],
+        out_specs=[VMEM] * 3,
         compiler_params=params(16),
         cost_estimate=pl.CostEstimate(
             flops=4 * vocab * groups * rows * embed, bytes_accessed=2**21, transcendentals=0
         ),
         name="pool",
-    )(place, feature_ids[0].T, tables[0])
+    )(feature_ids[0].T, cross_bias, tables[0])
     crossing = flip_over(send, "dp", 1)
     both = jnp.stack([keep, crossing], axis=1)
     held = [both[0]] + [flip_over(both[chip], "dp", 2 * chip) for chip in range(1, chips)]
-    terms = jnp.stack(split_three(cross_bias.reshape(-1))).reshape(-1, embed)
-    bias_rows = -(-terms.shape[0] // SUBLANES) * SUBLANES
-    terms = jnp.pad(terms, ((0, bias_rows - terms.shape[0]), (0, 0)))
     piece = jnp.concatenate([part.reshape(-1, embed) for part in held] + [terms])
 
     got = jnp.stack([leg for leg in legs])
-    own = [got] + [flip_over(got, "dp", 2 * chip) for chip in range(1, chips)]
+    own = spread(got)
     other = [flip_over(own[chip], "dp", 1) for chip in range(chips)]
-    pieces = [piece] + [shift_over(piece, "mp", step) for step in steps]
+    pieces = [piece] + [flip_over(piece, "mp", step) for step in steps]
 
     tower_own = [tower_weight] + [
         flip_over(tower_weight, "dp", 2 * chip) for chip in range(1, chips)
@@ -309,13 +312,13 @@
 
     samples = rows * members
     units = tower_weight.shape[1]
-    inputs = [place, table_of_feature, cross_down, cross_up, cross_bias]
+    inputs = [table_of_feature, cross_down, cross_up]
     inputs += [tower_bias.reshape(1, units)]
     inputs += own + other + tower_own + tower_other + pieces
     return pl.pallas_call(
         functools.partial(cross_kernel, members, chips),
         out_shape=jax.ShapeDtypeStruct((samples, units), jnp.bfloat16),
-        in_specs=[SMEM, SMEM] + [VMEM] * (len(inputs) - 2),
+        in_specs=[SMEM] + [VMEM] * (len(inputs) - 1),
         out_specs=VMEM,
         scratch_shapes=[
             pltpu.VMEM((samples, width), jnp.bfloat16),
@@ -343,7 +346,7 @@
         rows = feature_ids.shape[1] // (groups * members)
         fits = 4 * cross_down.size * members <= GATHER_LIMIT
         fits = fits and block % tables.shape[2] == 0 and block % (SUBLANES * groups) == 0
-        fits = fits and (rows == LANES // 2 or rows % LANES == 0) and groups & (groups - 1) == 0
+        fits = fits and (rows == LANES // 2 or rows % LANES == 0) and groups == 2 * PLANE and members & (members - 1) == 0
         return (gather_body if fits else reduce_body)(*args)
 
     return jax.shard_map(

time: 59.7 us -> 58.6 us (0.982)
  starting transfers between devices: 24.3 us -> 26.6 us
  waiting for transfers between devices: 24.7 us -> 22.5 us
  Pallas kernels: 8 us -> 6.99 us
    ppermute x18 -> x21, starting transfers between devices: 12.1 us -> 23 us  [flip_over(): return lax.ppermute(value, axis, [(i, i ^ mask) for i in range(count)])]
    ppermute x6 -> x3, starting transfers between devices: 12.2 us -> 3.58 us  [by_role(): return lax.ppermute(value, axis, pairs)]
    ppermute x6 -> x3, waiting for transfers between devices: 8.38 us -> 0.01 us  [by_role(): return lax.ppermute(value, axis, pairs)]
    ppermute x18 -> x21, waiting for transfers between devices: 16.4 us -> 22.4 us  [flip_over(): return lax.ppermute(value, axis, [(i, i ^ mask) for i in range(count)])]
    pallas_call x1, Pallas kernels: 4.74 us -> 3.7 us  [gather_body(): pl.pallas_call(functools.partial(pool_kernel, 256), out_shape=[jax.ShapeD...]
    unnamed x21 -> x20, local copies, waits for them, and re-layouts: 1.29 us -> 1.29 us
  transfers between devices with their start and end apart: 24 -> 24, of which waited for: 9 -> 8; matrix products, arithmetic and copies ran while one was open for 0% -> 0% of each run, Pallas kernels for 8% -> 6%
where the time goes in v2:
time: 58.6 us; the launch traced here: 58.4 us
  starting transfers between devices  26.6 us (45%)
  waiting for transfers between devices  22.5 us (38%)
  Pallas kernels  6.99 us (12%)
  local copies, waits for them, and re-layouts  2.12 us (4%)
    ppermute x21, starting transfers between devices, flip_over(): return lax.ppermute(value, axis, [(i, i ^ mask) for i in range(count)])  23 us
    ppermute x21, waiting for transfers between devices, flip_over(): return lax.ppermute(value, axis, [(i, i ^ mask) for i in range(count)])  22.4 us
    pallas_call x1, Pallas kernels, gather_body(): pl.pallas_call(functools.partial(pool_kernel, 256), out_shape=[jax.ShapeD...  3.7 us
    ppermute x3, starting transfers between devices, by_role(): return lax.ppermute(value, axis, pairs)  3.58 us
    pallas_call x1, Pallas kernels, gather_body(): pl.pallas_call(functools.partial(cross_kernel, members, chips), out_shape...  3.29 us
    unnamed x20, local copies, waits for them, and re-layouts  1.29 us
  transfers between devices with their start and end apart: 24, of which 8 were waited for; matrix products, arithmetic and copies ran while one was open for 0% of the time, Pallas kernels for 6%

profile of v2, /device:TPU:0, one launch (start us, length us, event | category | flops | bytes accessed | tf_op | source)
XLA Modules:
  0.0 58.4 jit_solution(16379007190386343813)
XLA Ops:
  0.0 0.8 %dynamic-slice_bitcast_fusion.2 = (bf16[32,512]{1,0:T(8,128)(2,1)S(1)}, bf16[32,512]{1,0:T(8,128)(2,1)S(1)}, bf16[32,512]{1,0:T(8,128)(2,1)S(1)}, bf16[32,512]{1,0:T(8,128)(2,1)S(1)}) fusion(bf16[2,256,512]{2,1,0:T(8,128)(2,1)} %refs_2_.1, s32[]{:T(128)S(6)} %select_n.4, s32[]{:T(128)S(6)} %add.5, bf16[2,256,512]{2,1,0:T(8,128)(2,1)} %refs_1_.1), kind=kLoop, calls=%fused_computation.17 | loop fusion | bytes 262152 | tf_op jit(solution)/shard_map/squeeze | solution.py:280
  0.9 5.1 %collective-permute-start.2 = (bf16[128,512]{1,0:T(8,128)(2,1)S(1)}, bf16[128,512]{1,0:T(8,128)(2,1)S(1)}, u32[]{:S(2)}, u32[]{:S(2)}) collective-permute-start(bf16[128,512]{1,0:T(8,128)(2,1)S(1)} %pad_maximum_fusion.1), channel_id=1, source_target_pairs={{0,3},{1,2},{2,1},{3,0},{4,7},{5,6},{6,5},{7,4},{8,11},{9,10},{10,... | collective-permute-start | bytes 393224 | tf_op jit(solution)/shard_map/ppermute | solution.py:238
  6.0 0.6 %collective-permute-start = (bf16[128,512]{1,0:T(8,128)(2,1)S(1)}, bf16[128,512]{1,0:T(8,128)(2,1)S(1)}, u32[]{:S(2)}, u32[]{:S(2)}) collective-permute-start(bf16[128,512]{1,0:T(8,128)(2,1)S(1)} %pad_maximum_fusion.1), channel_id=1, source_target_pairs={{0,1},{1,0},{2,3},{3,2},{4,5},{5,4},{6,7},{7,6},{8,9},{9,8},{10,11... | collective-permute-start | bytes 393224 | tf_op jit(solution)/shard_map/ppermute | solution.py:238
  6.7 1.2 %copy-done.5 = bf16[1,4096,128]{2,1,0:T(8,128)(2,1)S(1)} copy-done((bf16[1,4096,128]{2,1,0:T(8,128)(2,1)S(1)}, bf16[1,4096,128]{2,1,0:T(8,128)(2,1)}, u32[]{:S(2)}) %copy-start.5) | copy-done | bytes 1048600
  7.9 3.7 %pool.1 = (bf16[4,64,128]{2,1,0:T(8,128)(2,1)S(1)}, bf16[4,64,128]{2,1,0:T(8,128)(2,1)S(1)}, bf16[16,128]{1,0:T(8,128)(2,1)S(1)}) custom-call(s32[8,2048]{1,0:T(8,128)S(1)} %bitcast.31, f32[2,256]{1,0:T(2,128)S(1)} %copy-done.7, bf16[4096,128]{1,0:T(8,128)(2,1)S(1)} %bitcast.30), custom_call_target="tpu_custom_call" | custom-call | flops 1073741824 | bytes 2097152 | tf_op jit(solution)/shard_map/pool/pallas_call | solution.py:286
  11.7 5.4 %collective-permute-done.1 = bf16[128,512]{1,0:T(8,128)(2,1)S(1)} collective-permute-done((bf16[128,512]{1,0:T(8,128)(2,1)S(1)}, bf16[128,512]{1,0:T(8,128)(2,1)S(1)}, u32[]{:S(2)}, u32[]{:S(2)}) %collective-permute-start.1) | collective-permute-done | bytes 131104 | tf_op jit(solution)/shard_map/ppermute | solution.py:238
  17.1 1.6 %collective-permute-start.3 = (bf16[3,128,512]{2,1,0:T(8,128)(2,1)S(1)}, bf16[3,128,512]{2,1,0:T(8,128)(2,1)S(1)}, u32[]{:S(2)}, u32[]{:S(2)}) collective-permute-start(bf16[3,128,512]{2,1,0:T(8,128)(2,1)S(1)} %pad_maximum_fusion.refs_4_), channel_id=1, source_target_pairs={{0,8},{4,20},{8,0},{12,28},{16,24},{20,4},{24,16},{28,12},{1,9},{5... | collective-permute-start | bytes 1179656 | tf_op jit(solution)/shard_map/ppermute | solution.py:244
  18.7 1.5 %collective-permute-start.12 = (bf16[128,512]{1,0:T(8,128)(2,1)S(1)}, bf16[128,512]{1,0:T(8,128)(2,1)S(1)}, u32[]{:S(2)}, u32[]{:S(2)}) collective-permute-start(bf16[128,512]{1,0:T(8,128)(2,1)S(1)} %copy-done.2), channel_id=1, source_target_pairs={{0,24},{4,28},{8,16},{12,20},{16,8},{20,12},{24,0},{28,4},{1,25},{... | collective-permute-start | bytes 393224 | tf_op jit(solution)/shard_map/ppermute | solution.py:238
  20.7 2.5 %collective-permute-start.20 = (bf16[2,64,128]{2,1,0:T(8,128)(2,1)S(1)}, bf16[2,64,128]{2,1,0:T(8,128)(2,1)S(1)}, u32[]{:S(2)}, u32[]{:S(2)}) collective-permute-start(bf16[2,64,128]{2,1,0:T(8,128)(2,1)S(1)} %get-tuple-element.15), channel_id=1, source_target_pairs={{0,24},{4,28},{8,16},{12,20},{16,8},{20,12},{24,0},{28,4},{1,25},{... | collective-permute-start | bytes 98312 | tf_op jit(solution)/shard_map/ppermute | solution.py:238
  23.2 0.5 collective-permute-start.18
  23.8 4.9 %collective-permute-done.18 = bf16[2,64,128]{2,1,0:T(8,128)(2,1)S(1)} collective-permute-done((bf16[2,64,128]{2,1,0:T(8,128)(2,1)S(1)}, bf16[2,64,128]{2,1,0:T(8,128)(2,1)S(1)}, u32[]{:S(2)}, u32[]{:S(2)}) %collective-permute-start.18) | collective-permute-done | bytes 32800 | tf_op jit(solution)/shard_map/ppermute | solution.py:238
  28.6 1.5 %collective-permute-start.19 = (bf16[2,64,128]{2,1,0:T(8,128)(2,1)S(1)}, bf16[2,64,128]{2,1,0:T(8,128)(2,1)S(1)}, u32[]{:S(2)}, u32[]{:S(2)}) collective-permute-start(bf16[2,64,128]{2,1,0:T(8,128)(2,1)S(1)} %get-tuple-element.18), channel_id=1, source_target_pairs={{0,16},{4,20},{8,24},{12,28},{16,0},{20,4},{24,8},{28,12},{1,17},{... | collective-permute-start | bytes 98312 | tf_op jit(solution)/shard_map/ppermute | solution.py:238
  30.2 2.4 %collective-permute-done.19 = bf16[2,64,128]{2,1,0:T(8,128)(2,1)S(1)} collective-permute-done((bf16[2,64,128]{2,1,0:T(8,128)(2,1)S(1)}, bf16[2,64,128]{2,1,0:T(8,128)(2,1)S(1)}, u32[]{:S(2)}, u32[]{:S(2)}) %collective-permute-start.19) | collective-permute-done | bytes 32800 | tf_op jit(solution)/shard_map/ppermute | solution.py:238
  32.5 1.5 %collective-permute-start.4 = (bf16[3,128,512]{2,1,0:T(8,128)(2,1)S(1)}, bf16[3,128,512]{2,1,0:T(8,128)(2,1)S(1)}, u32[]{:S(2)}, u32[]{:S(2)}) collective-permute-start(bf16[3,128,512]{2,1,0:T(8,128)(2,1)S(1)} %pad_maximum_fusion.refs_4_), channel_id=1, source_target_pairs={{0,16},{4,12},{8,24},{12,4},{16,0},{20,28},{24,8},{28,20},{1,17},{... | collective-permute-start | bytes 1179656 | tf_op jit(solution)/shard_map/ppermute | solution.py:244
  34.6 1.6 %collective-permute-start.10 = (bf16[128,512]{1,0:T(8,128)(2,1)S(1)}, bf16[128,512]{1,0:T(8,128)(2,1)S(1)}, u32[]{:S(2)}, u32[]{:S(2)}) collective-permute-start(bf16[128,512]{1,0:T(8,128)(2,1)S(1)} %copy-done.2), channel_id=1, source_target_pairs={{0,8},{4,12},{8,0},{12,4},{16,24},{20,28},{24,16},{28,20},{1,9},{5... | collective-permute-start | bytes 393224 | tf_op jit(solution)/shard_map/ppermute | solution.py:238
  36.2 2.4 %collective-permute-start.23 = (bf16[528,128]{1,0:T(8,128)(2,1)S(1)}, bf16[528,128]{1,0:T(8,128)(2,1)S(1)}, u32[]{:S(2)}, u32[]{:S(2)}) collective-permute-start(bf16[528,128]{1,0:T(8,128)(2,1)S(1)} %constant_dynamic-update-slice_fusion.refs_20_), channel_id=1, source_target_pairs={{0,3},{1,2},{2,1},{3,0},{4,7},{5,6},{6,5},{7,4},{8,11},{9,10},{10,... | collective-permute-start | bytes 405512 | tf_op jit(solution)/shard_map/ppermute | solution.py:238
  38.6 2.5 %collective-permute-done.10.refs_13_ = bf16[128,512]{1,0:T(8,128)(2,1)S(1)} collective-permute-done((bf16[128,512]{1,0:T(8,128)(2,1)S(1)}, bf16[128,512]{1,0:T(8,128)(2,1)S(1)}, u32[]{:S(2)}, u32[]{:S(2)}) %collective-permute-start.10) | collective-permute-done | bytes 131104 | tf_op jit(solution)/shard_map/ppermute | solution.py:238
  41.0 2.9 %collective-permute-start.21 = (bf16[528,128]{1,0:T(8,128)(2,1)S(1)}, bf16[528,128]{1,0:T(8,128)(2,1)S(1)}, u32[]{:S(2)}, u32[]{:S(2)}) collective-permute-start(bf16[528,128]{1,0:T(8,128)(2,1)S(1)} %constant_dynamic-update-slice_fusion.refs_20_), channel_id=1, source_target_pairs={{0,1},{1,0},{2,3},{3,2},{4,5},{5,4},{6,7},{7,6},{8,9},{9,8},{10,11... | collective-permute-start | bytes 405512 | tf_op jit(solution)/shard_map/ppermute | solution.py:238
  44.1 1.8 %collective-permute-start.6 = (bf16[3,128,512]{2,1,0:T(8,128)(2,1)S(1)}, bf16[3,128,512]{2,1,0:T(8,128)(2,1)S(1)}, u32[]{:S(2)}, u32[]{:S(2)}) collective-permute-start(bf16[3,128,512]{2,1,0:T(8,128)(2,1)S(1)} %pad_maximum_fusion.refs_4_), channel_id=1, source_target_pairs={{0,4},{4,0},{8,12},{12,8},{16,20},{20,16},{24,28},{28,24},{1,5},{5... | collective-permute-start | bytes 1179656 | tf_op jit(solution)/shard_map/ppermute | solution.py:238
  45.9 4.2 %collective-permute-done.22.refs_22_ = bf16[528,128]{1,0:T(8,128)(2,1)S(1)} collective-permute-done((bf16[528,128]{1,0:T(8,128)(2,1)S(1)}, bf16[528,128]{1,0:T(8,128)(2,1)S(1)}, u32[]{:S(2)}, u32[]{:S(2)}) %collective-permute-start.22) | collective-permute-done | bytes 135200 | tf_op jit(solution)/shard_map/ppermute | solution.py:238
  50.5 0.6 collective-permute-start.7
  51.8 1.9 %collective-permute-done.15.refs_18_ = bf16[128,512]{1,0:T(8,128)(2,1)S(1)} collective-permute-done((bf16[128,512]{1,0:T(8,128)(2,1)S(1)}, bf16[128,512]{1,0:T(8,128)(2,1)S(1)}, u32[]{:S(2)}, u32[]{:S(2)}) %collective-permute-start.15) | collective-permute-done | bytes 131104 | tf_op jit(solution)/shard_map/ppermute | solution.py:238
  54.1 1.0 %collective-permute-done.14.refs_17_ = bf16[128,512]{1,0:T(8,128)(2,1)S(1)} collective-permute-done((bf16[128,512]{1,0:T(8,128)(2,1)S(1)}, bf16[128,512]{1,0:T(8,128)(2,1)S(1)}, u32[]{:S(2)}, u32[]{:S(2)}) %collective-permute-start.14) | collective-permute-done | bytes 131104 | tf_op jit(solution)/shard_map/ppermute | solution.py:238
  55.1 3.3 %cross.1 = bf16[256,512]{1,0:T(8,128)(2,1)} custom-call(s32[8]{0:T(128)S(1)} %copy-done.4, bf16[2,256,512]{2,1,0:T(8,128)(2,1)S(1)} %copy-done, bf16[2,256,512]{2,1,0:T(8,128)(2,1)S(1)} %copy-done.1, f32[1,512]{1,0:T(1,128)S(1)} %bitcast.29, bf16[3,128,512]{2,1,0:T(8,128)(2,1)S(1)} %pad_maximum_fusion.refs_4_, ...), custom_call_target="tpu_custom_call" | custom-call | flops 1342177280 | bytes 8388608 | tf_op jit(solution)/shard_map/cross/pallas_call | solution.py:318
  (51 shorter events, 3.1 us)
Async XLA Ops:
  0.9 10.8 %collective-permute-start.2 = (bf16[128,512]{1,0:T(8,128)(2,1)S(1)}, bf16[128,512]{1,0:T(8,128)(2,1)S(1)}, u32[]{:S(2)}, u32[]{:S(2)}) collective-permute-start(bf16[128,512]{1,0:T(8,128)(2,1)S(1)} %pad_maximum_fusion.1), channel_id=1, source_target_pairs={{0,3},{1,2},{2,1},{3,0},{4,7},{5,6},{6,5},{7,4},{8,11},{9,10},{10,... | collective-permute-start | bytes 393224 | tf_op jit(solution)/shard_map/ppermute | solution.py:238
  6.0 11.1 %collective-permute-start.1 = (bf16[128,512]{1,0:T(8,128)(2,1)S(1)}, bf16[128,512]{1,0:T(8,128)(2,1)S(1)}, u32[]{:S(2)}, u32[]{:S(2)}) collective-permute-start(bf16[128,512]{1,0:T(8,128)(2,1)S(1)} %pad_maximum_fusion.1), channel_id=1, source_target_pairs={{0,2},{1,3},{2,0},{3,1},{4,6},{5,7},{6,4},{7,5},{8,10},{9,11},{10,... | collective-permute-start | bytes 393224 | tf_op jit(solution)/shard_map/ppermute | solution.py:238
  6.0 11.1 %collective-permute-start = (bf16[128,512]{1,0:T(8,128)(2,1)S(1)}, bf16[128,512]{1,0:T(8,128)(2,1)S(1)}, u32[]{:S(2)}, u32[]{:S(2)}) collective-permute-start(bf16[128,512]{1,0:T(8,128)(2,1)S(1)} %pad_maximum_fusion.1), channel_id=1, source_target_pairs={{0,1},{1,0},{2,3},{3,2},{4,5},{5,4},{6,7},{7,6},{8,9},{9,8},{10,11... | collective-permute-start | bytes 393224 | tf_op jit(solution)/shard_map/ppermute | solution.py:238
  11.6 9.1 %collective-permute-start.17 = (bf16[4,64,128]{2,1,0:T(8,128)(2,1)S(1)}, bf16[4,64,128]{2,1,0:T(8,128)(2,1)S(1)}, u32[]{:S(2)}, u32[]{:S(2)}) collective-permute-start(bf16[4,64,128]{2,1,0:T(8,128)(2,1)S(1)} %get-tuple-element.9), channel_id=1, source_target_pairs={{0,4},{4,0},{8,12},{12,8},{16,20},{20,16},{24,28},{28,24},{1,5},{5... | collective-permute-start | bytes 196616 | tf_op jit(solution)/shard_map/ppermute | solution.py:238
  17.1 16.9 %collective-permute-start.3 = (bf16[3,128,512]{2,1,0:T(8,128)(2,1)S(1)}, bf16[3,128,512]{2,1,0:T(8,128)(2,1)S(1)}, u32[]{:S(2)}, u32[]{:S(2)}) collective-permute-start(bf16[3,128,512]{2,1,0:T(8,128)(2,1)S(1)} %pad_maximum_fusion.refs_4_), channel_id=1, source_target_pairs={{0,8},{4,20},{8,0},{12,28},{16,24},{20,4},{24,16},{28,12},{1,9},{5... | collective-permute-start | bytes 1179656 | tf_op jit(solution)/shard_map/ppermute | solution.py:244
  18.7 17.4 %collective-permute-start.12 = (bf16[128,512]{1,0:T(8,128)(2,1)S(1)}, bf16[128,512]{1,0:T(8,128)(2,1)S(1)}, u32[]{:S(2)}, u32[]{:S(2)}) collective-permute-start(bf16[128,512]{1,0:T(8,128)(2,1)S(1)} %copy-done.2), channel_id=1, source_target_pairs={{0,24},{4,28},{8,16},{12,20},{16,8},{20,12},{24,0},{28,4},{1,25},{... | collective-permute-start | bytes 393224 | tf_op jit(solution)/shard_map/ppermute | solution.py:238
  20.2 16.0 %collective-permute-start.11 = (bf16[128,512]{1,0:T(8,128)(2,1)S(1)}, bf16[128,512]{1,0:T(8,128)(2,1)S(1)}, u32[]{:S(2)}, u32[]{:S(2)}) collective-permute-start(bf16[128,512]{1,0:T(8,128)(2,1)S(1)} %copy-done.2), channel_id=1, source_target_pairs={{0,16},{4,20},{8,24},{12,28},{16,0},{20,4},{24,8},{28,12},{1,17},{... | collective-permute-start | bytes 393224 | tf_op jit(solution)/shard_map/ppermute | solution.py:238
  20.7 13.9 %collective-permute-start.20 = (bf16[2,64,128]{2,1,0:T(8,128)(2,1)S(1)}, bf16[2,64,128]{2,1,0:T(8,128)(2,1)S(1)}, u32[]{:S(2)}, u32[]{:S(2)}) collective-permute-start(bf16[2,64,128]{2,1,0:T(8,128)(2,1)S(1)} %get-tuple-element.15), channel_id=1, source_target_pairs={{0,24},{4,28},{8,16},{12,20},{16,8},{20,12},{24,0},{28,4},{1,25},{... | collective-permute-start | bytes 98312 | tf_op jit(solution)/shard_map/ppermute | solution.py:238
  23.2 5.4 %collective-permute-start.18 = (bf16[2,64,128]{2,1,0:T(8,128)(2,1)S(1)}, bf16[2,64,128]{2,1,0:T(8,128)(2,1)S(1)}, u32[]{:S(2)}, u32[]{:S(2)}) collective-permute-start(bf16[2,64,128]{2,1,0:T(8,128)(2,1)S(1)} %get-tuple-element.17), channel_id=1, source_target_pairs={{0,8},{4,12},{8,0},{12,4},{16,24},{20,28},{24,16},{28,20},{1,9},{5... | collective-permute-start | bytes 98312 | tf_op jit(solution)/shard_map/ppermute | solution.py:238
  28.6 3.9 %collective-permute-start.19 = (bf16[2,64,128]{2,1,0:T(8,128)(2,1)S(1)}, bf16[2,64,128]{2,1,0:T(8,128)(2,1)S(1)}, u32[]{:S(2)}, u32[]{:S(2)}) collective-permute-start(bf16[2,64,128]{2,1,0:T(8,128)(2,1)S(1)} %get-tuple-element.18), channel_id=1, source_target_pairs={{0,16},{4,20},{8,24},{12,28},{16,0},{20,4},{24,8},{28,12},{1,17},{... | collective-permute-start | bytes 98312 | tf_op jit(solution)/shard_map/ppermute | solution.py:238
  32.5 18.5 %collective-permute-start.4 = (bf16[3,128,512]{2,1,0:T(8,128)(2,1)S(1)}, bf16[3,128,512]{2,1,0:T(8,128)(2,1)S(1)}, u32[]{:S(2)}, u32[]{:S(2)}) collective-permute-start(bf16[3,128,512]{2,1,0:T(8,128)(2,1)S(1)} %pad_maximum_fusion.refs_4_), channel_id=1, source_target_pairs={{0,16},{4,12},{8,24},{12,4},{16,0},{20,28},{24,8},{28,20},{1,17},{... | collective-permute-start | bytes 1179656 | tf_op jit(solution)/shard_map/ppermute | solution.py:244
  34.1 17.0 %collective-permute-start.5 = (bf16[3,128,512]{2,1,0:T(8,128)(2,1)S(1)}, bf16[3,128,512]{2,1,0:T(8,128)(2,1)S(1)}, u32[]{:S(2)}, u32[]{:S(2)}) collective-permute-start(bf16[3,128,512]{2,1,0:T(8,128)(2,1)S(1)} %collective-permute-done.3.refs_5_), channel_id=1, source_target_pairs={{0,16},{4,12},{8,24},{12,4},{16,0},{20,28},{24,8},{28,20},{1,17},{... | collective-permute-start | bytes 1179656 | tf_op jit(solution)/shard_map/ppermute | solution.py:244
  34.6 6.4 %collective-permute-start.10 = (bf16[128,512]{1,0:T(8,128)(2,1)S(1)}, bf16[128,512]{1,0:T(8,128)(2,1)S(1)}, u32[]{:S(2)}, u32[]{:S(2)}) collective-permute-start(bf16[128,512]{1,0:T(8,128)(2,1)S(1)} %copy-done.2), channel_id=1, source_target_pairs={{0,8},{4,12},{8,0},{12,4},{16,24},{20,28},{24,16},{28,20},{1,9},{5... | collective-permute-start | bytes 393224 | tf_op jit(solution)/shard_map/ppermute | solution.py:238
  36.1 4.9 %collective-permute-start.13 = (bf16[128,512]{1,0:T(8,128)(2,1)S(1)}, bf16[128,512]{1,0:T(8,128)(2,1)S(1)}, u32[]{:S(2)}, u32[]{:S(2)}) collective-permute-start(bf16[128,512]{1,0:T(8,128)(2,1)S(1)} %copy-done.2), channel_id=1, source_target_pairs={{0,4},{4,0},{8,12},{12,8},{16,20},{20,16},{24,28},{28,24},{1,5},{5... | collective-permute-start | bytes 393224 | tf_op jit(solution)/shard_map/ppermute | solution.py:238
  36.2 7.9 %collective-permute-start.23 = (bf16[528,128]{1,0:T(8,128)(2,1)S(1)}, bf16[528,128]{1,0:T(8,128)(2,1)S(1)}, u32[]{:S(2)}, u32[]{:S(2)}) collective-permute-start(bf16[528,128]{1,0:T(8,128)(2,1)S(1)} %constant_dynamic-update-slice_fusion.refs_20_), channel_id=1, source_target_pairs={{0,3},{1,2},{2,1},{3,0},{4,7},{5,6},{6,5},{7,4},{8,11},{9,10},{10,... | collective-permute-start | bytes 405512 | tf_op jit(solution)/shard_map/ppermute | solution.py:238
  41.0 9.1 %collective-permute-start.22 = (bf16[528,128]{1,0:T(8,128)(2,1)S(1)}, bf16[528,128]{1,0:T(8,128)(2,1)S(1)}, u32[]{:S(2)}, u32[]{:S(2)}) collective-permute-start(bf16[528,128]{1,0:T(8,128)(2,1)S(1)} %constant_dynamic-update-slice_fusion.refs_20_), channel_id=1, source_target_pairs={{0,2},{1,3},{2,0},{3,1},{4,6},{5,7},{6,4},{7,5},{8,10},{9,11},{10,... | collective-permute-start | bytes 405512 | tf_op jit(solution)/shard_map/ppermute | solution.py:238
  41.0 9.4 %collective-permute-start.21 = (bf16[528,128]{1,0:T(8,128)(2,1)S(1)}, bf16[528,128]{1,0:T(8,128)(2,1)S(1)}, u32[]{:S(2)}, u32[]{:S(2)}) collective-permute-start(bf16[528,128]{1,0:T(8,128)(2,1)S(1)} %constant_dynamic-update-slice_fusion.refs_20_), channel_id=1, source_target_pairs={{0,1},{1,0},{2,3},{3,2},{4,5},{5,4},{6,7},{7,6},{8,9},{9,8},{10,11... | collective-permute-start | bytes 405512 | tf_op jit(solution)/shard_map/ppermute | solution.py:238
  44.1 10.9 %collective-permute-start.6 = (bf16[3,128,512]{2,1,0:T(8,128)(2,1)S(1)}, bf16[3,128,512]{2,1,0:T(8,128)(2,1)S(1)}, u32[]{:S(2)}, u32[]{:S(2)}) collective-permute-start(bf16[3,128,512]{2,1,0:T(8,128)(2,1)S(1)} %pad_maximum_fusion.refs_4_), channel_id=1, source_target_pairs={{0,4},{4,0},{8,12},{12,8},{16,20},{20,16},{24,28},{28,24},{1,5},{5... | collective-permute-start | bytes 1179656 | tf_op jit(solution)/shard_map/ppermute | solution.py:238
  50.1 1.5 %collective-permute-start.16 = (bf16[128,512]{1,0:T(8,128)(2,1)S(1)}, bf16[128,512]{1,0:T(8,128)(2,1)S(1)}, u32[]{:S(2)}, u32[]{:S(2)}) collective-permute-start(bf16[128,512]{1,0:T(8,128)(2,1)S(1)} %collective-permute-done.12.refs_15_), channel_id=1, source_target_pairs={{0,4},{4,0},{8,12},{12,8},{16,20},{20,16},{24,28},{28,24},{1,5},{5... | collective-permute-start | bytes 393224 | tf_op jit(solution)/shard_map/ppermute | solution.py:238
  50.5 4.6 %collective-permute-start.7 = (bf16[3,128,512]{2,1,0:T(8,128)(2,1)S(1)}, bf16[3,128,512]{2,1,0:T(8,128)(2,1)S(1)}, u32[]{:S(2)}, u32[]{:S(2)}) collective-permute-start(bf16[3,128,512]{2,1,0:T(8,128)(2,1)S(1)} %collective-permute-done.3.refs_5_), channel_id=1, source_target_pairs={{0,4},{4,0},{8,12},{12,8},{16,20},{20,16},{24,28},{28,24},{1,5},{5... | collective-permute-start | bytes 1179656 | tf_op jit(solution)/shard_map/ppermute | solution.py:238
  51.0 4.0 %collective-permute-start.8 = (bf16[3,128,512]{2,1,0:T(8,128)(2,1)S(1)}, bf16[3,128,512]{2,1,0:T(8,128)(2,1)S(1)}, u32[]{:S(2)}, u32[]{:S(2)}) collective-permute-start(bf16[3,128,512]{2,1,0:T(8,128)(2,1)S(1)} %collective-permute-done.4.refs_6_), channel_id=1, source_target_pairs={{0,4},{4,0},{8,12},{12,8},{16,20},{20,16},{24,28},{28,24},{1,5},{5... | collective-permute-start | bytes 1179656 | tf_op jit(solution)/shard_map/ppermute | solution.py:238
  51.0 4.0 %collective-permute-start.9 = (bf16[3,128,512]{2,1,0:T(8,128)(2,1)S(1)}, bf16[3,128,512]{2,1,0:T(8,128)(2,1)S(1)}, u32[]{:S(2)}, u32[]{:S(2)}) collective-permute-start(bf16[3,128,512]{2,1,0:T(8,128)(2,1)S(1)} %collective-permute-done.5.refs_7_), channel_id=1, source_target_pairs={{0,4},{4,0},{8,12},{12,8},{16,20},{20,16},{24,28},{28,24},{1,5},{5... | collective-permute-start | bytes 1179656 | tf_op jit(solution)/shard_map/ppermute | solution.py:238
  51.5 2.1 %collective-permute-start.15 = (bf16[128,512]{1,0:T(8,128)(2,1)S(1)}, bf16[128,512]{1,0:T(8,128)(2,1)S(1)}, u32[]{:S(2)}, u32[]{:S(2)}) collective-permute-start(bf16[128,512]{1,0:T(8,128)(2,1)S(1)} %collective-permute-done.11.refs_14_), channel_id=1, source_target_pairs={{0,4},{4,0},{8,12},{12,8},{16,20},{20,16},{24,28},{28,24},{1,5},{5... | collective-permute-start | bytes 393224 | tf_op jit(solution)/shard_map/ppermute | solution.py:238
  53.7 1.4 %collective-permute-start.14 = (bf16[128,512]{1,0:T(8,128)(2,1)S(1)}, bf16[128,512]{1,0:T(8,128)(2,1)S(1)}, u32[]{:S(2)}, u32[]{:S(2)}) collective-permute-start(bf16[128,512]{1,0:T(8,128)(2,1)S(1)} %collective-permute-done.10.refs_13_), channel_id=1, source_target_pairs={{0,4},{4,0},{8,12},{12,8},{16,20},{20,16},{24,28},{28,24},{1,5},{5... | collective-permute-start | bytes 393224 | tf_op jit(solution)/shard_map/ppermute | solution.py:238
  (8 other events, 137.5 us)

commit v3 on v2

--- a/solution.py
+++ b/solution.py
@@ -12,6 +12,7 @@
 
 LANES = 128
 SUBLANES = 16
+CHUNK = 256
 PLANE = 4
 
 VMEM = pl.BlockSpec(memory_space=pltpu.VMEM)
@@ -77,8 +78,25 @@
     return pltpu.CompilerParams(vmem_limit_bytes=mib * 2**20)
 
 
+def select_kernel(groups, ids_ref, own_ref):
+    batch = ids_ref.shape[1]
+    rows = own_ref.shape[1] // groups
+    per_group = batch // groups
+    member = lax.axis_index("mp")
+    wanted = []
+    for owner in range(groups):
+        if rows == LANES // 2:
+            at = pl.multiple_of(owner * per_group + lax.div(member, 2) * LANES, LANES)
+            wide = ids_ref[:, pl.ds(at, LANES)]
+            wanted.append(jnp.where(lax.rem(member, 2) == 0, wide[:, :rows], wide[:, rows:]))
+        else:
+            at = pl.multiple_of(owner * per_group + member * rows, LANES)
+            wanted.append(ids_ref[:, pl.ds(at, rows)])
+    own_ref[...] = jnp.concatenate(wanted, axis=1)
+
+
 def pool_kernel(
-    chunk, ids_ref, bias_ref, table_ref, keep_ref, send_ref, terms_ref
+    chunk, ids_ref, bias_ref, table_ref, keep_ref, send_ref, terms_ref, marks_ref
 ):
     vocab, embed = table_ref.shape
     rest = bias_ref[...]
@@ -93,31 +111,25 @@
                     layer : layer + 1, part * embed : (part + 1) * embed
                 ]
         rest = rest - rounded.astype(jnp.float32)
-    hots, batch = ids_ref.shape
+    hots = ids_ref.shape[0]
     chips, rows, _ = keep_ref.shape
     groups = 2 * chips
     samples = groups * rows
-    per_group = batch // groups
-    group, member = lax.axis_index("dp"), lax.axis_index("mp")
-    wanted = []
-    for owner in range(groups):
-        if rows == LANES // 2:
-            at = pl.multiple_of(owner * per_group + lax.div(member, 2) * LANES, LANES)
-            wide = ids_ref[:, pl.ds(at, LANES)]
-            wanted.append(jnp.where(lax.rem(member, 2) == 0, wide[:, :rows], wide[:, rows:]))
-        else:
-            at = pl.multiple_of(owner * per_group + member * rows, LANES)
-            wanted.append(ids_ref[:, pl.ds(at, rows)])
-    ids = jnp.concatenate(wanted, axis=1)
+    group = lax.axis_index("dp")
+    ids = ids_ref[...]
     total = jnp.zeros((embed, samples), jnp.float32)
     row_at = lax.broadcasted_iota(jnp.int16, (chunk, samples), 0)
     one = jnp.ones((), jnp.bfloat16)
     zero = jnp.zeros((), jnp.bfloat16)
+    low = (ids & (chunk - 1)).astype(jnp.int16)
+    high = lax.shift_right_logical(ids, chunk.bit_length() - 1)
+    for hot in range(hots):
+        marks_ref[hot] = jnp.where(low[hot : hot + 1, :] == row_at, one, zero)
     for start in range(0, vocab, chunk):
-        shifted = (ids - start).astype(jnp.int16)
+        inside = jnp.where(high == start // chunk, 1.0, 0.0).astype(jnp.bfloat16)
         counts = None
         for hot in range(hots):
-            term = jnp.where(shifted[hot : hot + 1, :] == row_at, one, zero)
+            term = marks_ref[hot] * inside[hot : hot + 1, :]
             counts = term if counts is None else counts + term
         total = total + lax.dot_general(
             table_ref[start : start + chunk, :],
@@ -264,7 +276,7 @@
     groups = lax.axis_size("dp")
     members = lax.axis_size("mp")
     group = lax.axis_index("dp")
-    _, batch, _ = feature_ids.shape
+    _, batch, hots = feature_ids.shape
     rows = batch // (groups * members)
     _, vocab, embed = tables.shape
     layers, block, rank = cross_down.shape
@@ -283,18 +295,30 @@
 
     bias_rows = -(-3 * cross_bias.size // embed // SUBLANES) * SUBLANES
 
+    own_ids = pl.pallas_call(
+        functools.partial(select_kernel, groups),
+        out_shape=jax.ShapeDtypeStruct((hots, groups * rows), jnp.int32),
+        in_specs=[VMEM],
+        out_specs=VMEM,
+        compiler_params=params(2),
+        cost_estimate=pl.CostEstimate(
+            flops=4 * 10**9, bytes_accessed=2**17, transcendentals=0
+        ),
+        name="select",
+    )(feature_ids[0].T)
     keep, send, terms = pl.pallas_call(
-        functools.partial(pool_kernel, 256),
+        functools.partial(pool_kernel, CHUNK),
         out_shape=[jax.ShapeDtypeStruct((chips, rows, embed), jnp.bfloat16)] * 2
         + [jax.ShapeDtypeStruct((bias_rows, embed), jnp.bfloat16)],
         in_specs=[VMEM, VMEM, VMEM],
         out_specs=[VMEM] * 3,
+        scratch_shapes=[pltpu.VMEM((hots, CHUNK, groups * rows), jnp.bfloat16)],
         compiler_params=params(16),
         cost_estimate=pl.CostEstimate(
             flops=4 * vocab * groups * rows * embed, bytes_accessed=2**21, transcendentals=0
         ),
         name="pool",
-    )(feature_ids[0].T, cross_bias, tables[0])
+    )(own_ids, cross_bias, tables[0])
     crossing = flip_over(send, "dp", 1)
     both = jnp.stack([keep, crossing], axis=1)
     held = [both[0]] + [flip_over(both[chip], "dp", 2 * chip) for chip in range(1, chips)]
@@ -346,7 +370,7 @@
         rows = feature_ids.shape[1] // (groups * members)
         fits = 4 * cross_down.size * members <= GATHER_LIMIT
         fits = fits and block % tables.shape[2] == 0 and block % (SUBLANES * groups) == 0
-        fits = fits and (rows == LANES // 2 or rows % LANES == 0) and groups == 2 * PLANE and members & (members - 1) == 0
+        fits = fits and (rows == LANES // 2 or rows % LANES == 0) and groups == 2 * PLANE and tables.shape[1] % CHUNK == 0 and members & (members - 1) == 0
         return (gather_body if fits else reduce_body)(*args)
 
     return jax.shard_map(

time: 58.6 us -> 58.6 us (level)
  waiting for transfers between devices: 22.5 us -> 23.1 us
    ppermute x21, waiting for transfers between devices: 22.4 us -> 23.1 us  [flip_over(): return lax.ppermute(value, axis, [(i, i ^ mask) for i in range(count)])]
    pallas_call x1 -> x2, Pallas kernels: 3.7 us -> 3.15 us  [the longest x1 3.01 us: gather_body(): pl.pallas_call(functools.partial(pool_kernel, CHUNK), out_shape=[jax.Shap...]
  transfers between devices with their start and end apart: 24 -> 24, of which waited for: 8 -> 8; matrix products, arithmetic and copies ran while one was open for 0% -> 0% of each run, Pallas kernels for 6% -> 5%
where the time goes in v3:
time: 58.6 us; the launch traced here: 58.4 us
  starting transfers between devices  26.6 us (45%)
  waiting for transfers between devices  23.1 us (39%)
  Pallas kernels  6.45 us (11%)
  local copies, waits for them, and re-layouts  1.97 us (3%)
    ppermute x21, waiting for transfers between devices, flip_over(): return lax.ppermute(value, axis, [(i, i ^ mask) for i in range(count)])  23.1 us
    ppermute x21, starting transfers between devices, flip_over(): return lax.ppermute(value, axis, [(i, i ^ mask) for i in range(count)])  23 us
    ppermute x3, starting transfers between devices, by_role(): return lax.ppermute(value, axis, pairs)  3.58 us
    pallas_call x1, Pallas kernels, gather_body(): pl.pallas_call(functools.partial(cross_kernel, members, chips), out_shape...  3.3 us
    pallas_call x1, Pallas kernels, gather_body(): pl.pallas_call(functools.partial(pool_kernel, CHUNK), out_shape=[jax.Shap...  3.01 us
  transfers between devices with their start and end apart: 24, of which 8 were waited for; matrix products, arithmetic and copies ran while one was open for 0% of the time, Pallas kernels for 5%

profile of v3, /device:TPU:0, one launch (start us, length us, event | category | flops | bytes accessed | tf_op | source)
XLA Modules:
  0.0 58.4 jit_solution(17346718961754371035)
XLA Ops:
  0.0 0.8 %dynamic-slice_bitcast_fusion.2 = (bf16[32,512]{1,0:T(8,128)(2,1)S(1)}, bf16[32,512]{1,0:T(8,128)(2,1)S(1)}, bf16[32,512]{1,0:T(8,128)(2,1)S(1)}, bf16[32,512]{1,0:T(8,128)(2,1)S(1)}) fusion(bf16[2,256,512]{2,1,0:T(8,128)(2,1)} %refs_2_.1, s32[]{:T(128)S(6)} %select_n.4, s32[]{:T(128)S(6)} %add.5, bf16[2,256,512]{2,1,0:T(8,128)(2,1)} %refs_1_.1), kind=kLoop, calls=%fused_computation.17 | loop fusion | bytes 262152 | tf_op jit(solution)/shard_map/squeeze | solution.py:292
  0.9 5.1 %collective-permute-start.2 = (bf16[128,512]{1,0:T(8,128)(2,1)S(1)}, bf16[128,512]{1,0:T(8,128)(2,1)S(1)}, u32[]{:S(2)}, u32[]{:S(2)}) collective-permute-start(bf16[128,512]{1,0:T(8,128)(2,1)S(1)} %pad_maximum_fusion.1), channel_id=1, source_target_pairs={{0,3},{1,2},{2,1},{3,0},{4,7},{5,6},{6,5},{7,4},{8,11},{9,10},{10,... | collective-permute-start | bytes 393224 | tf_op jit(solution)/shard_map/ppermute | solution.py:250
  6.0 0.6 %collective-permute-start = (bf16[128,512]{1,0:T(8,128)(2,1)S(1)}, bf16[128,512]{1,0:T(8,128)(2,1)S(1)}, u32[]{:S(2)}, u32[]{:S(2)}) collective-permute-start(bf16[128,512]{1,0:T(8,128)(2,1)S(1)} %pad_maximum_fusion.1), channel_id=1, source_target_pairs={{0,1},{1,0},{2,3},{3,2},{4,5},{5,4},{6,7},{7,6},{8,9},{9,8},{10,11... | collective-permute-start | bytes 393224 | tf_op jit(solution)/shard_map/ppermute | solution.py:250
  6.8 1.1 %copy-done.5 = bf16[1,4096,128]{2,1,0:T(8,128)(2,1)S(1)} copy-done((bf16[1,4096,128]{2,1,0:T(8,128)(2,1)S(1)}, bf16[1,4096,128]{2,1,0:T(8,128)(2,1)}, u32[]{:S(2)}) %copy-start.5) | copy-done | bytes 1048600
  7.9 3.0 %pool.1 = (bf16[4,64,128]{2,1,0:T(8,128)(2,1)S(1)}, bf16[4,64,128]{2,1,0:T(8,128)(2,1)S(1)}, bf16[16,128]{1,0:T(8,128)(2,1)S(1)}) custom-call(s32[8,512]{1,0:T(8,128)S(1)} %select.1.ids_ref, f32[2,256]{1,0:T(2,128)S(1)} %copy-done.7, bf16[4096,128]{1,0:T(8,128)(2,1)S(1)} %bitcast.30), custom_call_target="tpu_custom_call" | custom-call | flops 1073741824 | bytes 2097152 | tf_op jit(solution)/shard_map/pool/pallas_call | solution.py:309
  11.0 6.1 %collective-permute-done.1 = bf16[128,512]{1,0:T(8,128)(2,1)S(1)} collective-permute-done((bf16[128,512]{1,0:T(8,128)(2,1)S(1)}, bf16[128,512]{1,0:T(8,128)(2,1)S(1)}, u32[]{:S(2)}, u32[]{:S(2)}) %collective-permute-start.1) | collective-permute-done | bytes 131104 | tf_op jit(solution)/shard_map/ppermute | solution.py:250
  17.1 1.6 %collective-permute-start.3 = (bf16[3,128,512]{2,1,0:T(8,128)(2,1)S(1)}, bf16[3,128,512]{2,1,0:T(8,128)(2,1)S(1)}, u32[]{:S(2)}, u32[]{:S(2)}) collective-permute-start(bf16[3,128,512]{2,1,0:T(8,128)(2,1)S(1)} %pad_maximum_fusion.refs_4_), channel_id=1, source_target_pairs={{0,8},{4,20},{8,0},{12,28},{16,24},{20,4},{24,16},{28,12},{1,9},{5... | collective-permute-start | bytes 1179656 | tf_op jit(solution)/shard_map/ppermute | solution.py:256
  18.7 1.5 %collective-permute-start.12 = (bf16[128,512]{1,0:T(8,128)(2,1)S(1)}, bf16[128,512]{1,0:T(8,128)(2,1)S(1)}, u32[]{:S(2)}, u32[]{:S(2)}) collective-permute-start(bf16[128,512]{1,0:T(8,128)(2,1)S(1)} %copy-done.2), channel_id=1, source_target_pairs={{0,24},{4,28},{8,16},{12,20},{16,8},{20,12},{24,0},{28,4},{1,25},{... | collective-permute-start | bytes 393224 | tf_op jit(solution)/shard_map/ppermute | solution.py:250
  20.7 2.5 %collective-permute-start.20 = (bf16[2,64,128]{2,1,0:T(8,128)(2,1)S(1)}, bf16[2,64,128]{2,1,0:T(8,128)(2,1)S(1)}, u32[]{:S(2)}, u32[]{:S(2)}) collective-permute-start(bf16[2,64,128]{2,1,0:T(8,128)(2,1)S(1)} %get-tuple-element.15), channel_id=1, source_target_pairs={{0,24},{4,28},{8,16},{12,20},{16,8},{20,12},{24,0},{28,4},{1,25},{... | collective-permute-start | bytes 98312 | tf_op jit(solution)/shard_map/ppermute | solution.py:250
  23.2 0.5 collective-permute-start.18
  23.8 4.9 %collective-permute-done.18 = bf16[2,64,128]{2,1,0:T(8,128)(2,1)S(1)} collective-permute-done((bf16[2,64,128]{2,1,0:T(8,128)(2,1)S(1)}, bf16[2,64,128]{2,1,0:T(8,128)(2,1)S(1)}, u32[]{:S(2)}, u32[]{:S(2)}) %collective-permute-start.18) | collective-permute-done | bytes 32800 | tf_op jit(solution)/shard_map/ppermute | solution.py:250
  28.6 1.5 %collective-permute-start.19 = (bf16[2,64,128]{2,1,0:T(8,128)(2,1)S(1)}, bf16[2,64,128]{2,1,0:T(8,128)(2,1)S(1)}, u32[]{:S(2)}, u32[]{:S(2)}) collective-permute-start(bf16[2,64,128]{2,1,0:T(8,128)(2,1)S(1)} %get-tuple-element.18), channel_id=1, source_target_pairs={{0,16},{4,20},{8,24},{12,28},{16,0},{20,4},{24,8},{28,12},{1,17},{... | collective-permute-start | bytes 98312 | tf_op jit(solution)/shard_map/ppermute | solution.py:250
  30.1 2.4 %collective-permute-done.19 = bf16[2,64,128]{2,1,0:T(8,128)(2,1)S(1)} collective-permute-done((bf16[2,64,128]{2,1,0:T(8,128)(2,1)S(1)}, bf16[2,64,128]{2,1,0:T(8,128)(2,1)S(1)}, u32[]{:S(2)}, u32[]{:S(2)}) %collective-permute-start.19) | collective-permute-done | bytes 32800 | tf_op jit(solution)/shard_map/ppermute | solution.py:250
  32.5 1.5 %collective-permute-start.4 = (bf16[3,128,512]{2,1,0:T(8,128)(2,1)S(1)}, bf16[3,128,512]{2,1,0:T(8,128)(2,1)S(1)}, u32[]{:S(2)}, u32[]{:S(2)}) collective-permute-start(bf16[3,128,512]{2,1,0:T(8,128)(2,1)S(1)} %pad_maximum_fusion.refs_4_), channel_id=1, source_target_pairs={{0,16},{4,12},{8,24},{12,4},{16,0},{20,28},{24,8},{28,20},{1,17},{... | collective-permute-start | bytes 1179656 | tf_op jit(solution)/shard_map/ppermute | solution.py:256
  34.6 1.6 %collective-permute-start.10 = (bf16[128,512]{1,0:T(8,128)(2,1)S(1)}, bf16[128,512]{1,0:T(8,128)(2,1)S(1)}, u32[]{:S(2)}, u32[]{:S(2)}) collective-permute-start(bf16[128,512]{1,0:T(8,128)(2,1)S(1)} %copy-done.2), channel_id=1, source_target_pairs={{0,8},{4,12},{8,0},{12,4},{16,24},{20,28},{24,16},{28,20},{1,9},{5... | collective-permute-start | bytes 393224 | tf_op jit(solution)/shard_map/ppermute | solution.py:250
  36.2 2.4 %collective-permute-start.23 = (bf16[528,128]{1,0:T(8,128)(2,1)S(1)}, bf16[528,128]{1,0:T(8,128)(2,1)S(1)}, u32[]{:S(2)}, u32[]{:S(2)}) collective-permute-start(bf16[528,128]{1,0:T(8,128)(2,1)S(1)} %constant_dynamic-update-slice_fusion.refs_20_), channel_id=1, source_target_pairs={{0,3},{1,2},{2,1},{3,0},{4,7},{5,6},{6,5},{7,4},{8,11},{9,10},{10,... | collective-permute-start | bytes 405512 | tf_op jit(solution)/shard_map/ppermute | solution.py:250
  38.5 2.5 %collective-permute-done.10.refs_13_ = bf16[128,512]{1,0:T(8,128)(2,1)S(1)} collective-permute-done((bf16[128,512]{1,0:T(8,128)(2,1)S(1)}, bf16[128,512]{1,0:T(8,128)(2,1)S(1)}, u32[]{:S(2)}, u32[]{:S(2)}) %collective-permute-start.10) | collective-permute-done | bytes 131104 | tf_op jit(solution)/shard_map/ppermute | solution.py:250
  41.0 2.9 %collective-permute-start.21 = (bf16[528,128]{1,0:T(8,128)(2,1)S(1)}, bf16[528,128]{1,0:T(8,128)(2,1)S(1)}, u32[]{:S(2)}, u32[]{:S(2)}) collective-permute-start(bf16[528,128]{1,0:T(8,128)(2,1)S(1)} %constant_dynamic-update-slice_fusion.refs_20_), channel_id=1, source_target_pairs={{0,1},{1,0},{2,3},{3,2},{4,5},{5,4},{6,7},{7,6},{8,9},{9,8},{10,11... | collective-permute-start | bytes 405512 | tf_op jit(solution)/shard_map/ppermute | solution.py:250
  44.1 1.8 %collective-permute-start.6 = (bf16[3,128,512]{2,1,0:T(8,128)(2,1)S(1)}, bf16[3,128,512]{2,1,0:T(8,128)(2,1)S(1)}, u32[]{:S(2)}, u32[]{:S(2)}) collective-permute-start(bf16[3,128,512]{2,1,0:T(8,128)(2,1)S(1)} %pad_maximum_fusion.refs_4_), channel_id=1, source_target_pairs={{0,4},{4,0},{8,12},{12,8},{16,20},{20,16},{24,28},{28,24},{1,5},{5... | collective-permute-start | bytes 1179656 | tf_op jit(solution)/shard_map/ppermute | solution.py:250
  45.9 4.2 %collective-permute-done.22.refs_22_ = bf16[528,128]{1,0:T(8,128)(2,1)S(1)} collective-permute-done((bf16[528,128]{1,0:T(8,128)(2,1)S(1)}, bf16[528,128]{1,0:T(8,128)(2,1)S(1)}, u32[]{:S(2)}, u32[]{:S(2)}) %collective-permute-start.22) | collective-permute-done | bytes 135200 | tf_op jit(solution)/shard_map/ppermute | solution.py:250
  50.5 0.6 collective-permute-start.7
  51.8 1.9 %collective-permute-done.15.refs_18_ = bf16[128,512]{1,0:T(8,128)(2,1)S(1)} collective-permute-done((bf16[128,512]{1,0:T(8,128)(2,1)S(1)}, bf16[128,512]{1,0:T(8,128)(2,1)S(1)}, u32[]{:S(2)}, u32[]{:S(2)}) %collective-permute-start.15) | collective-permute-done | bytes 131104 | tf_op jit(solution)/shard_map/ppermute | solution.py:250
  54.0 1.0 %collective-permute-done.14.refs_17_ = bf16[128,512]{1,0:T(8,128)(2,1)S(1)} collective-permute-done((bf16[128,512]{1,0:T(8,128)(2,1)S(1)}, bf16[128,512]{1,0:T(8,128)(2,1)S(1)}, u32[]{:S(2)}, u32[]{:S(2)}) %collective-permute-start.14) | collective-permute-done | bytes 131104 | tf_op jit(solution)/shard_map/ppermute | solution.py:250
  55.1 3.3 %cross.1 = bf16[256,512]{1,0:T(8,128)(2,1)} custom-call(s32[8]{0:T(128)S(1)} %copy-done.4, bf16[2,256,512]{2,1,0:T(8,128)(2,1)S(1)} %copy-done, bf16[2,256,512]{2,1,0:T(8,128)(2,1)S(1)} %copy-done.1, f32[1,512]{1,0:T(1,128)S(1)} %bitcast.29, bf16[3,128,512]{2,1,0:T(8,128)(2,1)S(1)} %pad_maximum_fusion.refs_4_, ...), custom_call_target="tpu_custom_call" | custom-call | flops 1342177280 | bytes 8388608 | tf_op jit(solution)/shard_map/cross/pallas_call | solution.py:342
  (52 shorter events, 3.2 us)
Async XLA Ops:
  0.9 10.1 %collective-permute-start.2 = (bf16[128,512]{1,0:T(8,128)(2,1)S(1)}, bf16[128,512]{1,0:T(8,128)(2,1)S(1)}, u32[]{:S(2)}, u32[]{:S(2)}) collective-permute-start(bf16[128,512]{1,0:T(8,128)(2,1)S(1)} %pad_maximum_fusion.1), channel_id=1, source_target_pairs={{0,3},{1,2},{2,1},{3,0},{4,7},{5,6},{6,5},{7,4},{8,11},{9,10},{10,... | collective-permute-start | bytes 393224 | tf_op jit(solution)/shard_map/ppermute | solution.py:250
  6.0 11.1 %collective-permute-start.1 = (bf16[128,512]{1,0:T(8,128)(2,1)S(1)}, bf16[128,512]{1,0:T(8,128)(2,1)S(1)}, u32[]{:S(2)}, u32[]{:S(2)}) collective-permute-start(bf16[128,512]{1,0:T(8,128)(2,1)S(1)} %pad_maximum_fusion.1), channel_id=1, source_target_pairs={{0,2},{1,3},{2,0},{3,1},{4,6},{5,7},{6,4},{7,5},{8,10},{9,11},{10,... | collective-permute-start | bytes 393224 | tf_op jit(solution)/shard_map/ppermute | solution.py:250
  6.0 11.1 %collective-permute-start = (bf16[128,512]{1,0:T(8,128)(2,1)S(1)}, bf16[128,512]{1,0:T(8,128)(2,1)S(1)}, u32[]{:S(2)}, u32[]{:S(2)}) collective-permute-start(bf16[128,512]{1,0:T(8,128)(2,1)S(1)} %pad_maximum_fusion.1), channel_id=1, source_target_pairs={{0,1},{1,0},{2,3},{3,2},{4,5},{5,4},{6,7},{7,6},{8,9},{9,8},{10,11... | collective-permute-start | bytes 393224 | tf_op jit(solution)/shard_map/ppermute | solution.py:250
  10.9 9.8 %collective-permute-start.17 = (bf16[4,64,128]{2,1,0:T(8,128)(2,1)S(1)}, bf16[4,64,128]{2,1,0:T(8,128)(2,1)S(1)}, u32[]{:S(2)}, u32[]{:S(2)}) collective-permute-start(bf16[4,64,128]{2,1,0:T(8,128)(2,1)S(1)} %get-tuple-element.9), channel_id=1, source_target_pairs={{0,4},{4,0},{8,12},{12,8},{16,20},{20,16},{24,28},{28,24},{1,5},{5... | collective-permute-start | bytes 196616 | tf_op jit(solution)/shard_map/ppermute | solution.py:250
  17.1 16.9 %collective-permute-start.3 = (bf16[3,128,512]{2,1,0:T(8,128)(2,1)S(1)}, bf16[3,128,512]{2,1,0:T(8,128)(2,1)S(1)}, u32[]{:S(2)}, u32[]{:S(2)}) collective-permute-start(bf16[3,128,512]{2,1,0:T(8,128)(2,1)S(1)} %pad_maximum_fusion.refs_4_), channel_id=1, source_target_pairs={{0,8},{4,20},{8,0},{12,28},{16,24},{20,4},{24,16},{28,12},{1,9},{5... | collective-permute-start | bytes 1179656 | tf_op jit(solution)/shard_map/ppermute | solution.py:256
  18.7 17.4 %collective-permute-start.12 = (bf16[128,512]{1,0:T(8,128)(2,1)S(1)}, bf16[128,512]{1,0:T(8,128)(2,1)S(1)}, u32[]{:S(2)}, u32[]{:S(2)}) collective-permute-start(bf16[128,512]{1,0:T(8,128)(2,1)S(1)} %copy-done.2), channel_id=1, source_target_pairs={{0,24},{4,28},{8,16},{12,20},{16,8},{20,12},{24,0},{28,4},{1,25},{... | collective-permute-start | bytes 393224 | tf_op jit(solution)/shard_map/ppermute | solution.py:250
  20.2 16.0 %collective-permute-start.11 = (bf16[128,512]{1,0:T(8,128)(2,1)S(1)}, bf16[128,512]{1,0:T(8,128)(2,1)S(1)}, u32[]{:S(2)}, u32[]{:S(2)}) collective-permute-start(bf16[128,512]{1,0:T(8,128)(2,1)S(1)} %copy-done.2), channel_id=1, source_target_pairs={{0,16},{4,20},{8,24},{12,28},{16,0},{20,4},{24,8},{28,12},{1,17},{... | collective-permute-start | bytes 393224 | tf_op jit(solution)/shard_map/ppermute | solution.py:250
  20.7 13.9 %collective-permute-start.20 = (bf16[2,64,128]{2,1,0:T(8,128)(2,1)S(1)}, bf16[2,64,128]{2,1,0:T(8,128)(2,1)S(1)}, u32[]{:S(2)}, u32[]{:S(2)}) collective-permute-start(bf16[2,64,128]{2,1,0:T(8,128)(2,1)S(1)} %get-tuple-element.15), channel_id=1, source_target_pairs={{0,24},{4,28},{8,16},{12,20},{16,8},{20,12},{24,0},{28,4},{1,25},{... | collective-permute-start | bytes 98312 | tf_op jit(solution)/shard_map/ppermute | solution.py:250
  23.2 5.4 %collective-permute-start.18 = (bf16[2,64,128]{2,1,0:T(8,128)(2,1)S(1)}, bf16[2,64,128]{2,1,0:T(8,128)(2,1)S(1)}, u32[]{:S(2)}, u32[]{:S(2)}) collective-permute-start(bf16[2,64,128]{2,1,0:T(8,128)(2,1)S(1)} %get-tuple-element.17), channel_id=1, source_target_pairs={{0,8},{4,12},{8,0},{12,4},{16,24},{20,28},{24,16},{28,20},{1,9},{5... | collective-permute-start | bytes 98312 | tf_op jit(solution)/shard_map/ppermute | solution.py:250
  28.6 3.9 %collective-permute-start.19 = (bf16[2,64,128]{2,1,0:T(8,128)(2,1)S(1)}, bf16[2,64,128]{2,1,0:T(8,128)(2,1)S(1)}, u32[]{:S(2)}, u32[]{:S(2)}) collective-permute-start(bf16[2,64,128]{2,1,0:T(8,128)(2,1)S(1)} %get-tuple-element.18), channel_id=1, source_target_pairs={{0,16},{4,20},{8,24},{12,28},{16,0},{20,4},{24,8},{28,12},{1,17},{... | collective-permute-start | bytes 98312 | tf_op jit(solution)/shard_map/ppermute | solution.py:250
  32.5 18.5 %collective-permute-start.4 = (bf16[3,128,512]{2,1,0:T(8,128)(2,1)S(1)}, bf16[3,128,512]{2,1,0:T(8,128)(2,1)S(1)}, u32[]{:S(2)}, u32[]{:S(2)}) collective-permute-start(bf16[3,128,512]{2,1,0:T(8,128)(2,1)S(1)} %pad_maximum_fusion.refs_4_), channel_id=1, source_target_pairs={{0,16},{4,12},{8,24},{12,4},{16,0},{20,28},{24,8},{28,20},{1,17},{... | collective-permute-start | bytes 1179656 | tf_op jit(solution)/shard_map/ppermute | solution.py:256
  34.0 17.0 %collective-permute-start.5 = (bf16[3,128,512]{2,1,0:T(8,128)(2,1)S(1)}, bf16[3,128,512]{2,1,0:T(8,128)(2,1)S(1)}, u32[]{:S(2)}, u32[]{:S(2)}) collective-permute-start(bf16[3,128,512]{2,1,0:T(8,128)(2,1)S(1)} %collective-permute-done.3.refs_5_), channel_id=1, source_target_pairs={{0,16},{4,12},{8,24},{12,4},{16,0},{20,28},{24,8},{28,20},{1,17},{... | collective-permute-start | bytes 1179656 | tf_op jit(solution)/shard_map/ppermute | solution.py:256
  34.6 6.4 %collective-permute-start.10 = (bf16[128,512]{1,0:T(8,128)(2,1)S(1)}, bf16[128,512]{1,0:T(8,128)(2,1)S(1)}, u32[]{:S(2)}, u32[]{:S(2)}) collective-permute-start(bf16[128,512]{1,0:T(8,128)(2,1)S(1)} %copy-done.2), channel_id=1, source_target_pairs={{0,8},{4,12},{8,0},{12,4},{16,24},{20,28},{24,16},{28,20},{1,9},{5... | collective-permute-start | bytes 393224 | tf_op jit(solution)/shard_map/ppermute | solution.py:250
  36.1 4.9 %collective-permute-start.13 = (bf16[128,512]{1,0:T(8,128)(2,1)S(1)}, bf16[128,512]{1,0:T(8,128)(2,1)S(1)}, u32[]{:S(2)}, u32[]{:S(2)}) collective-permute-start(bf16[128,512]{1,0:T(8,128)(2,1)S(1)} %copy-done.2), channel_id=1, source_target_pairs={{0,4},{4,0},{8,12},{12,8},{16,20},{20,16},{24,28},{28,24},{1,5},{5... | collective-permute-start | bytes 393224 | tf_op jit(solution)/shard_map/ppermute | solution.py:250
  36.2 7.9 %collective-permute-start.23 = (bf16[528,128]{1,0:T(8,128)(2,1)S(1)}, bf16[528,128]{1,0:T(8,128)(2,1)S(1)}, u32[]{:S(2)}, u32[]{:S(2)}) collective-permute-start(bf16[528,128]{1,0:T(8,128)(2,1)S(1)} %constant_dynamic-update-slice_fusion.refs_20_), channel_id=1, source_target_pairs={{0,3},{1,2},{2,1},{3,0},{4,7},{5,6},{6,5},{7,4},{8,11},{9,10},{10,... | collective-permute-start | bytes 405512 | tf_op jit(solution)/shard_map/ppermute | solution.py:250
  41.0 9.1 %collective-permute-start.22 = (bf16[528,128]{1,0:T(8,128)(2,1)S(1)}, bf16[528,128]{1,0:T(8,128)(2,1)S(1)}, u32[]{:S(2)}, u32[]{:S(2)}) collective-permute-start(bf16[528,128]{1,0:T(8,128)(2,1)S(1)} %constant_dynamic-update-slice_fusion.refs_20_), channel_id=1, source_target_pairs={{0,2},{1,3},{2,0},{3,1},{4,6},{5,7},{6,4},{7,5},{8,10},{9,11},{10,... | collective-permute-start | bytes 405512 | tf_op jit(solution)/shard_map/ppermute | solution.py:250
  41.0 9.4 %collective-permute-start.21 = (bf16[528,128]{1,0:T(8,128)(2,1)S(1)}, bf16[528,128]{1,0:T(8,128)(2,1)S(1)}, u32[]{:S(2)}, u32[]{:S(2)}) collective-permute-start(bf16[528,128]{1,0:T(8,128)(2,1)S(1)} %constant_dynamic-update-slice_fusion.refs_20_), channel_id=1, source_target_pairs={{0,1},{1,0},{2,3},{3,2},{4,5},{5,4},{6,7},{7,6},{8,9},{9,8},{10,11... | collective-permute-start | bytes 405512 | tf_op jit(solution)/shard_map/ppermute | solution.py:250
  44.1 10.9 %collective-permute-start.6 = (bf16[3,128,512]{2,1,0:T(8,128)(2,1)S(1)}, bf16[3,128,512]{2,1,0:T(8,128)(2,1)S(1)}, u32[]{:S(2)}, u32[]{:S(2)}) collective-permute-start(bf16[3,128,512]{2,1,0:T(8,128)(2,1)S(1)} %pad_maximum_fusion.refs_4_), channel_id=1, source_target_pairs={{0,4},{4,0},{8,12},{12,8},{16,20},{20,16},{24,28},{28,24},{1,5},{5... | collective-permute-start | bytes 1179656 | tf_op jit(solution)/shard_map/ppermute | solution.py:250
  50.1 1.5 %collective-permute-start.16 = (bf16[128,512]{1,0:T(8,128)(2,1)S(1)}, bf16[128,512]{1,0:T(8,128)(2,1)S(1)}, u32[]{:S(2)}, u32[]{:S(2)}) collective-permute-start(bf16[128,512]{1,0:T(8,128)(2,1)S(1)} %collective-permute-done.12.refs_15_), channel_id=1, source_target_pairs={{0,4},{4,0},{8,12},{12,8},{16,20},{20,16},{24,28},{28,24},{1,5},{5... | collective-permute-start | bytes 393224 | tf_op jit(solution)/shard_map/ppermute | solution.py:250
  50.5 4.6 %collective-permute-start.7 = (bf16[3,128,512]{2,1,0:T(8,128)(2,1)S(1)}, bf16[3,128,512]{2,1,0:T(8,128)(2,1)S(1)}, u32[]{:S(2)}, u32[]{:S(2)}) collective-permute-start(bf16[3,128,512]{2,1,0:T(8,128)(2,1)S(1)} %collective-permute-done.3.refs_5_), channel_id=1, source_target_pairs={{0,4},{4,0},{8,12},{12,8},{16,20},{20,16},{24,28},{28,24},{1,5},{5... | collective-permute-start | bytes 1179656 | tf_op jit(solution)/shard_map/ppermute | solution.py:250
  51.0 4.0 %collective-permute-start.8 = (bf16[3,128,512]{2,1,0:T(8,128)(2,1)S(1)}, bf16[3,128,512]{2,1,0:T(8,128)(2,1)S(1)}, u32[]{:S(2)}, u32[]{:S(2)}) collective-permute-start(bf16[3,128,512]{2,1,0:T(8,128)(2,1)S(1)} %collective-permute-done.4.refs_6_), channel_id=1, source_target_pairs={{0,4},{4,0},{8,12},{12,8},{16,20},{20,16},{24,28},{28,24},{1,5},{5... | collective-permute-start | bytes 1179656 | tf_op jit(solution)/shard_map/ppermute | solution.py:250
  51.0 4.0 %collective-permute-start.9 = (bf16[3,128,512]{2,1,0:T(8,128)(2,1)S(1)}, bf16[3,128,512]{2,1,0:T(8,128)(2,1)S(1)}, u32[]{:S(2)}, u32[]{:S(2)}) collective-permute-start(bf16[3,128,512]{2,1,0:T(8,128)(2,1)S(1)} %collective-permute-done.5.refs_7_), channel_id=1, source_target_pairs={{0,4},{4,0},{8,12},{12,8},{16,20},{20,16},{24,28},{28,24},{1,5},{5... | collective-permute-start | bytes 1179656 | tf_op jit(solution)/shard_map/ppermute | solution.py:250
  51.5 2.1 %collective-permute-start.15 = (bf16[128,512]{1,0:T(8,128)(2,1)S(1)}, bf16[128,512]{1,0:T(8,128)(2,1)S(1)}, u32[]{:S(2)}, u32[]{:S(2)}) collective-permute-start(bf16[128,512]{1,0:T(8,128)(2,1)S(1)} %collective-permute-done.11.refs_14_), channel_id=1, source_target_pairs={{0,4},{4,0},{8,12},{12,8},{16,20},{20,16},{24,28},{28,24},{1,5},{5... | collective-permute-start | bytes 393224 | tf_op jit(solution)/shard_map/ppermute | solution.py:250
  53.7 1.4 %collective-permute-start.14 = (bf16[128,512]{1,0:T(8,128)(2,1)S(1)}, bf16[128,512]{1,0:T(8,128)(2,1)S(1)}, u32[]{:S(2)}, u32[]{:S(2)}) collective-permute-start(bf16[128,512]{1,0:T(8,128)(2,1)S(1)} %collective-permute-done.10.refs_13_), channel_id=1, source_target_pairs={{0,4},{4,0},{8,12},{12,8},{16,20},{20,16},{24,28},{28,24},{1,5},{5... | collective-permute-start | bytes 393224 | tf_op jit(solution)/shard_map/ppermute | solution.py:250
  (8 other events, 132.9 us)

commit v4 on v3

--- a/solution.py
+++ b/solution.py
@@ -161,7 +161,7 @@
     tower_own_refs, tower_other_refs = take(chips), take(chips)
     piece_refs = take(members)
     (hidden_ref,) = take(1)
-    embedded_ref, bias_full, down_full, up_full, tower_full = take(5)
+    embedded_ref, bias_full, down_full, up_full, tower_full, done_ref, written = take(7)
 
     group, member = lax.axis_index("dp"), lax.axis_index("mp")
     layers, block, _ = down_ref.shape
@@ -196,12 +196,8 @@
     own_slots = [jnp.bitwise_xor(group, mask) for mask in (0, near, far, 6)]
     other_slots = [jnp.bitwise_xor(group, mask) for mask in (1, far + 1, near + 1, 7)]
 
-    for chip in range(chips):
-        for side, source in enumerate((tower_own_refs[chip], tower_other_refs[chip])):
-            slot = jnp.bitwise_xor(group, 2 * chip + side)
-            depth = source.shape[0]
-            tower_full[pl.ds(pl.multiple_of(slot * depth, depth), depth), :] = source[...]
-
+    embedded = embedded_ref[...]
+    crossed = embedded
     for layer in range(layers):
         down_full[layer, pl.ds(base, block), :] = down_ref[layer]
         up_full[layer, pl.ds(base, block), :] = up_ref[layer]
@@ -218,10 +214,6 @@
                     up_full[layer, pl.ds(at, slice_rows), :] = source[
                         step - 1, first + slice_rows : first + 2 * slice_rows
                     ]
-
-    embedded = embedded_ref[...]
-    crossed = embedded
-    for layer in range(layers):
         projected = jnp.dot(
             crossed, down_full[layer], preferred_element_type=jnp.float32
         ).astype(jnp.bfloat16)
@@ -236,13 +228,30 @@
             + crossed.astype(jnp.float32)
         ).astype(jnp.bfloat16)
 
-    pre_act = jnp.dot(crossed, tower_full[...], preferred_element_type=jnp.float32)
-    hidden = jnp.maximum(pre_act + tower_bias_ref[...], 0.0).astype(jnp.bfloat16)
-    for step in range(members):
-        owner = jnp.bitwise_xor(member, step)
-        hidden_ref[pl.ds(pl.multiple_of(owner * rows, rows), rows), :] = hidden[
-            step * rows : (step + 1) * rows
-        ]
+    for chip in range(chips):
+        for side, source in enumerate((tower_own_refs[chip], tower_other_refs[chip])):
+            slot = jnp.bitwise_xor(group, 2 * chip + side)
+            depth = source.shape[0]
+            tower_full[pl.ds(pl.multiple_of(slot * depth, depth), depth), :] = source[...]
+    units = tower_full.shape[1]
+    part = units // 2
+    copies = []
+    for index in range(2):
+        columns = slice(index * part, (index + 1) * part)
+        pre_act = jnp.dot(crossed, tower_full[:, columns], preferred_element_type=jnp.float32)
+        hidden = jnp.maximum(pre_act + tower_bias_ref[:, columns], 0.0).astype(jnp.bfloat16)
+        for step in range(members):
+            owner = jnp.bitwise_xor(member, step)
+            done_ref[index, pl.ds(pl.multiple_of(owner * rows, rows), rows), :] = hidden[
+                step * rows : (step + 1) * rows
+            ]
+        copy = pltpu.make_async_copy(
+            done_ref.at[index], hidden_ref.at[:, pl.ds(index * part, part)], written.at[index]
+        )
+        copy.start()
+        copies.append(copy)
+    for copy in copies:
+        copy.wait()
 
 
 def flip_over(value, axis, mask):
@@ -343,13 +352,15 @@
         functools.partial(cross_kernel, members, chips),
         out_shape=jax.ShapeDtypeStruct((samples, units), jnp.bfloat16),
         in_specs=[SMEM] + [VMEM] * (len(inputs) - 1),
-        out_specs=VMEM,
+        out_specs=pl.BlockSpec(memory_space=pl.ANY),
         scratch_shapes=[
             pltpu.VMEM((samples, width), jnp.bfloat16),
             pltpu.VMEM((layers, width), jnp.float32),
             pltpu.VMEM((layers, width, rank), jnp.bfloat16),
             pltpu.VMEM((layers, width, rank), jnp.bfloat16),
             pltpu.VMEM((width, units), jnp.bfloat16),
+            pltpu.VMEM((2, samples, units // 2), jnp.bfloat16),
+            pltpu.SemaphoreType.DMA((2,)),
         ],
         compiler_params=params(32),
         cost_estimate=pl.CostEstimate(

time: 58.6 us -> 58.6 us (level)
  no operation moved by 1% of the time
where the time goes in v4:
time: 58.6 us; the launch traced here: 58.3 us
  starting transfers between devices  26.6 us (45%)
  waiting for transfers between devices  23.1 us (39%)
  Pallas kernels  6.4 us (11%)
  local copies, waits for them, and re-layouts  1.97 us (3%)
    ppermute x21, waiting for transfers between devices, flip_over(): return lax.ppermute(value, axis, [(i, i ^ mask) for i in range(count)])  23.1 us
    ppermute x21, starting transfers between devices, flip_over(): return lax.ppermute(value, axis, [(i, i ^ mask) for i in range(count)])  23 us
    ppermute x3, starting transfers between devices, by_role(): return lax.ppermute(value, axis, pairs)  3.58 us
    pallas_call x1, Pallas kernels, gather_body(): pl.pallas_call(functools.partial(cross_kernel, members, chips), out_shape...  3.25 us
    pallas_call x1, Pallas kernels, gather_body(): pl.pallas_call(functools.partial(pool_kernel, CHUNK), out_shape=[jax.Shap...  3.01 us
  transfers between devices with their start and end apart: 24, of which 8 were waited for; matrix products, arithmetic and copies ran while one was open for 0% of the time, Pallas kernels for 5%

profile of v4, /device:TPU:0, one launch (start us, length us, event | category | flops | bytes accessed | tf_op | source)
XLA Modules:
  0.0 58.3 jit_solution(3738410675089399207)
XLA Ops:
  0.0 0.8 %dynamic-slice_bitcast_fusion.2 = (bf16[32,512]{1,0:T(8,128)(2,1)S(1)}, bf16[32,512]{1,0:T(8,128)(2,1)S(1)}, bf16[32,512]{1,0:T(8,128)(2,1)S(1)}, bf16[32,512]{1,0:T(8,128)(2,1)S(1)}) fusion(bf16[2,256,512]{2,1,0:T(8,128)(2,1)} %refs_2_.1, s32[]{:T(128)S(6)} %select_n.4, s32[]{:T(128)S(6)} %add.5, bf16[2,256,512]{2,1,0:T(8,128)(2,1)} %refs_1_.1), kind=kLoop, calls=%fused_computation.17 | loop fusion | bytes 262152 | tf_op jit(solution)/shard_map/squeeze | solution.py:301
  0.9 5.1 %collective-permute-start.2 = (bf16[128,512]{1,0:T(8,128)(2,1)S(1)}, bf16[128,512]{1,0:T(8,128)(2,1)S(1)}, u32[]{:S(2)}, u32[]{:S(2)}) collective-permute-start(bf16[128,512]{1,0:T(8,128)(2,1)S(1)} %pad_maximum_fusion.1), channel_id=1, source_target_pairs={{0,3},{1,2},{2,1},{3,0},{4,7},{5,6},{6,5},{7,4},{8,11},{9,10},{10,... | collective-permute-start | bytes 393224 | tf_op jit(solution)/shard_map/ppermute | solution.py:259
  6.0 0.6 %collective-permute-start = (bf16[128,512]{1,0:T(8,128)(2,1)S(1)}, bf16[128,512]{1,0:T(8,128)(2,1)S(1)}, u32[]{:S(2)}, u32[]{:S(2)}) collective-permute-start(bf16[128,512]{1,0:T(8,128)(2,1)S(1)} %pad_maximum_fusion.1), channel_id=1, source_target_pairs={{0,1},{1,0},{2,3},{3,2},{4,5},{5,4},{6,7},{7,6},{8,9},{9,8},{10,11... | collective-permute-start | bytes 393224 | tf_op jit(solution)/shard_map/ppermute | solution.py:259
  6.8 1.1 %copy-done.5 = bf16[1,4096,128]{2,1,0:T(8,128)(2,1)S(1)} copy-done((bf16[1,4096,128]{2,1,0:T(8,128)(2,1)S(1)}, bf16[1,4096,128]{2,1,0:T(8,128)(2,1)}, u32[]{:S(2)}) %copy-start.5) | copy-done | bytes 1048600
  7.9 3.0 %pool.1 = (bf16[4,64,128]{2,1,0:T(8,128)(2,1)S(1)}, bf16[4,64,128]{2,1,0:T(8,128)(2,1)S(1)}, bf16[16,128]{1,0:T(8,128)(2,1)S(1)}) custom-call(s32[8,512]{1,0:T(8,128)S(1)} %select.1.ids_ref, f32[2,256]{1,0:T(2,128)S(1)} %copy-done.7, bf16[4096,128]{1,0:T(8,128)(2,1)S(1)} %bitcast.30), custom_call_target="tpu_custom_call" | custom-call | flops 1073741824 | bytes 2097152 | tf_op jit(solution)/shard_map/pool/pallas_call | solution.py:318
  11.0 6.1 %collective-permute-done.1 = bf16[128,512]{1,0:T(8,128)(2,1)S(1)} collective-permute-done((bf16[128,512]{1,0:T(8,128)(2,1)S(1)}, bf16[128,512]{1,0:T(8,128)(2,1)S(1)}, u32[]{:S(2)}, u32[]{:S(2)}) %collective-permute-start.1) | collective-permute-done | bytes 131104 | tf_op jit(solution)/shard_map/ppermute | solution.py:259
  17.1 1.6 %collective-permute-start.3 = (bf16[3,128,512]{2,1,0:T(8,128)(2,1)S(1)}, bf16[3,128,512]{2,1,0:T(8,128)(2,1)S(1)}, u32[]{:S(2)}, u32[]{:S(2)}) collective-permute-start(bf16[3,128,512]{2,1,0:T(8,128)(2,1)S(1)} %pad_maximum_fusion.refs_4_), channel_id=1, source_target_pairs={{0,8},{4,20},{8,0},{12,28},{16,24},{20,4},{24,16},{28,12},{1,9},{5... | collective-permute-start | bytes 1179656 | tf_op jit(solution)/shard_map/ppermute | solution.py:265
  18.7 1.5 %collective-permute-start.12 = (bf16[128,512]{1,0:T(8,128)(2,1)S(1)}, bf16[128,512]{1,0:T(8,128)(2,1)S(1)}, u32[]{:S(2)}, u32[]{:S(2)}) collective-permute-start(bf16[128,512]{1,0:T(8,128)(2,1)S(1)} %copy-done.2), channel_id=1, source_target_pairs={{0,24},{4,28},{8,16},{12,20},{16,8},{20,12},{24,0},{28,4},{1,25},{... | collective-permute-start | bytes 393224 | tf_op jit(solution)/shard_map/ppermute | solution.py:259
  20.7 2.5 %collective-permute-start.20 = (bf16[2,64,128]{2,1,0:T(8,128)(2,1)S(1)}, bf16[2,64,128]{2,1,0:T(8,128)(2,1)S(1)}, u32[]{:S(2)}, u32[]{:S(2)}) collective-permute-start(bf16[2,64,128]{2,1,0:T(8,128)(2,1)S(1)} %get-tuple-element.15), channel_id=1, source_target_pairs={{0,24},{4,28},{8,16},{12,20},{16,8},{20,12},{24,0},{28,4},{1,25},{... | collective-permute-start | bytes 98312 | tf_op jit(solution)/shard_map/ppermute | solution.py:259
  23.2 0.5 collective-permute-start.18
  23.8 4.9 %collective-permute-done.18 = bf16[2,64,128]{2,1,0:T(8,128)(2,1)S(1)} collective-permute-done((bf16[2,64,128]{2,1,0:T(8,128)(2,1)S(1)}, bf16[2,64,128]{2,1,0:T(8,128)(2,1)S(1)}, u32[]{:S(2)}, u32[]{:S(2)}) %collective-permute-start.18) | collective-permute-done | bytes 32800 | tf_op jit(solution)/shard_map/ppermute | solution.py:259
  28.6 1.5 %collective-permute-start.19 = (bf16[2,64,128]{2,1,0:T(8,128)(2,1)S(1)}, bf16[2,64,128]{2,1,0:T(8,128)(2,1)S(1)}, u32[]{:S(2)}, u32[]{:S(2)}) collective-permute-start(bf16[2,64,128]{2,1,0:T(8,128)(2,1)S(1)} %get-tuple-element.18), channel_id=1, source_target_pairs={{0,16},{4,20},{8,24},{12,28},{16,0},{20,4},{24,8},{28,12},{1,17},{... | collective-permute-start | bytes 98312 | tf_op jit(solution)/shard_map/ppermute | solution.py:259
  30.1 2.4 %collective-permute-done.19 = bf16[2,64,128]{2,1,0:T(8,128)(2,1)S(1)} collective-permute-done((bf16[2,64,128]{2,1,0:T(8,128)(2,1)S(1)}, bf16[2,64,128]{2,1,0:T(8,128)(2,1)S(1)}, u32[]{:S(2)}, u32[]{:S(2)}) %collective-permute-start.19) | collective-permute-done | bytes 32800 | tf_op jit(solution)/shard_map/ppermute | solution.py:259
  32.5 1.5 %collective-permute-start.4 = (bf16[3,128,512]{2,1,0:T(8,128)(2,1)S(1)}, bf16[3,128,512]{2,1,0:T(8,128)(2,1)S(1)}, u32[]{:S(2)}, u32[]{:S(2)}) collective-permute-start(bf16[3,128,512]{2,1,0:T(8,128)(2,1)S(1)} %pad_maximum_fusion.refs_4_), channel_id=1, source_target_pairs={{0,16},{4,12},{8,24},{12,4},{16,0},{20,28},{24,8},{28,20},{1,17},{... | collective-permute-start | bytes 1179656 | tf_op jit(solution)/shard_map/ppermute | solution.py:265
  34.6 1.6 %collective-permute-start.10 = (bf16[128,512]{1,0:T(8,128)(2,1)S(1)}, bf16[128,512]{1,0:T(8,128)(2,1)S(1)}, u32[]{:S(2)}, u32[]{:S(2)}) collective-permute-start(bf16[128,512]{1,0:T(8,128)(2,1)S(1)} %copy-done.2), channel_id=1, source_target_pairs={{0,8},{4,12},{8,0},{12,4},{16,24},{20,28},{24,16},{28,20},{1,9},{5... | collective-permute-start | bytes 393224 | tf_op jit(solution)/shard_map/ppermute | solution.py:259
  36.2 2.4 %collective-permute-start.23 = (bf16[528,128]{1,0:T(8,128)(2,1)S(1)}, bf16[528,128]{1,0:T(8,128)(2,1)S(1)}, u32[]{:S(2)}, u32[]{:S(2)}) collective-permute-start(bf16[528,128]{1,0:T(8,128)(2,1)S(1)} %constant_dynamic-update-slice_fusion.refs_20_), channel_id=1, source_target_pairs={{0,3},{1,2},{2,1},{3,0},{4,7},{5,6},{6,5},{7,4},{8,11},{9,10},{10,... | collective-permute-start | bytes 405512 | tf_op jit(solution)/shard_map/ppermute | solution.py:259
  38.5 2.5 %collective-permute-done.10.refs_13_ = bf16[128,512]{1,0:T(8,128)(2,1)S(1)} collective-permute-done((bf16[128,512]{1,0:T(8,128)(2,1)S(1)}, bf16[128,512]{1,0:T(8,128)(2,1)S(1)}, u32[]{:S(2)}, u32[]{:S(2)}) %collective-permute-start.10) | collective-permute-done | bytes 131104 | tf_op jit(solution)/shard_map/ppermute | solution.py:259
  41.0 2.9 %collective-permute-start.21 = (bf16[528,128]{1,0:T(8,128)(2,1)S(1)}, bf16[528,128]{1,0:T(8,128)(2,1)S(1)}, u32[]{:S(2)}, u32[]{:S(2)}) collective-permute-start(bf16[528,128]{1,0:T(8,128)(2,1)S(1)} %constant_dynamic-update-slice_fusion.refs_20_), channel_id=1, source_target_pairs={{0,1},{1,0},{2,3},{3,2},{4,5},{5,4},{6,7},{7,6},{8,9},{9,8},{10,11... | collective-permute-start | bytes 405512 | tf_op jit(solution)/shard_map/ppermute | solution.py:259
  44.1 1.8 %collective-permute-start.6 = (bf16[3,128,512]{2,1,0:T(8,128)(2,1)S(1)}, bf16[3,128,512]{2,1,0:T(8,128)(2,1)S(1)}, u32[]{:S(2)}, u32[]{:S(2)}) collective-permute-start(bf16[3,128,512]{2,1,0:T(8,128)(2,1)S(1)} %pad_maximum_fusion.refs_4_), channel_id=1, source_target_pairs={{0,4},{4,0},{8,12},{12,8},{16,20},{20,16},{24,28},{28,24},{1,5},{5... | collective-permute-start | bytes 1179656 | tf_op jit(solution)/shard_map/ppermute | solution.py:259
  45.9 4.2 %collective-permute-done.22.refs_22_ = bf16[528,128]{1,0:T(8,128)(2,1)S(1)} collective-permute-done((bf16[528,128]{1,0:T(8,128)(2,1)S(1)}, bf16[528,128]{1,0:T(8,128)(2,1)S(1)}, u32[]{:S(2)}, u32[]{:S(2)}) %collective-permute-start.22) | collective-permute-done | bytes 135200 | tf_op jit(solution)/shard_map/ppermute | solution.py:259
  50.5 0.6 collective-permute-start.7
  51.8 1.9 %collective-permute-done.15.refs_18_ = bf16[128,512]{1,0:T(8,128)(2,1)S(1)} collective-permute-done((bf16[128,512]{1,0:T(8,128)(2,1)S(1)}, bf16[128,512]{1,0:T(8,128)(2,1)S(1)}, u32[]{:S(2)}, u32[]{:S(2)}) %collective-permute-start.15) | collective-permute-done | bytes 131104 | tf_op jit(solution)/shard_map/ppermute | solution.py:259
  54.0 1.0 %collective-permute-done.14.refs_17_ = bf16[128,512]{1,0:T(8,128)(2,1)S(1)} collective-permute-done((bf16[128,512]{1,0:T(8,128)(2,1)S(1)}, bf16[128,512]{1,0:T(8,128)(2,1)S(1)}, u32[]{:S(2)}, u32[]{:S(2)}) %collective-permute-start.14) | collective-permute-done | bytes 131104 | tf_op jit(solution)/shard_map/ppermute | solution.py:259
  55.1 3.2 %cross.1 = bf16[256,512]{1,0:T(8,128)(2,1)} custom-call(s32[8]{0:T(128)S(1)} %copy-done.4, bf16[2,256,512]{2,1,0:T(8,128)(2,1)S(1)} %copy-done, bf16[2,256,512]{2,1,0:T(8,128)(2,1)S(1)} %copy-done.1, f32[1,512]{1,0:T(1,128)S(1)} %bitcast.29, bf16[3,128,512]{2,1,0:T(8,128)(2,1)S(1)} %pad_maximum_fusion.refs_4_, ...), custom_call_target="tpu_custom_call" | custom-call | flops 1342177280 | bytes 8388608 | tf_op jit(solution)/shard_map/cross/pallas_call | solution.py:351
  (52 shorter events, 3.2 us)
Async XLA Ops:
  0.9 10.1 %collective-permute-start.2 = (bf16[128,512]{1,0:T(8,128)(2,1)S(1)}, bf16[128,512]{1,0:T(8,128)(2,1)S(1)}, u32[]{:S(2)}, u32[]{:S(2)}) collective-permute-start(bf16[128,512]{1,0:T(8,128)(2,1)S(1)} %pad_maximum_fusion.1), channel_id=1, source_target_pairs={{0,3},{1,2},{2,1},{3,0},{4,7},{5,6},{6,5},{7,4},{8,11},{9,10},{10,... | collective-permute-start | bytes 393224 | tf_op jit(solution)/shard_map/ppermute | solution.py:259
  6.0 11.1 %collective-permute-start.1 = (bf16[128,512]{1,0:T(8,128)(2,1)S(1)}, bf16[128,512]{1,0:T(8,128)(2,1)S(1)}, u32[]{:S(2)}, u32[]{:S(2)}) collective-permute-start(bf16[128,512]{1,0:T(8,128)(2,1)S(1)} %pad_maximum_fusion.1), channel_id=1, source_target_pairs={{0,2},{1,3},{2,0},{3,1},{4,6},{5,7},{6,4},{7,5},{8,10},{9,11},{10,... | collective-permute-start | bytes 393224 | tf_op jit(solution)/shard_map/ppermute | solution.py:259
  6.0 11.1 %collective-permute-start = (bf16[128,512]{1,0:T(8,128)(2,1)S(1)}, bf16[128,512]{1,0:T(8,128)(2,1)S(1)}, u32[]{:S(2)}, u32[]{:S(2)}) collective-permute-start(bf16[128,512]{1,0:T(8,128)(2,1)S(1)} %pad_maximum_fusion.1), channel_id=1, source_target_pairs={{0,1},{1,0},{2,3},{3,2},{4,5},{5,4},{6,7},{7,6},{8,9},{9,8},{10,11... | collective-permute-start | bytes 393224 | tf_op jit(solution)/shard_map/ppermute | solution.py:259
  10.9 9.8 %collective-permute-start.17 = (bf16[4,64,128]{2,1,0:T(8,128)(2,1)S(1)}, bf16[4,64,128]{2,1,0:T(8,128)(2,1)S(1)}, u32[]{:S(2)}, u32[]{:S(2)}) collective-permute-start(bf16[4,64,128]{2,1,0:T(8,128)(2,1)S(1)} %get-tuple-element.9), channel_id=1, source_target_pairs={{0,4},{4,0},{8,12},{12,8},{16,20},{20,16},{24,28},{28,24},{1,5},{5... | collective-permute-start | bytes 196616 | tf_op jit(solution)/shard_map/ppermute | solution.py:259
  17.1 16.9 %collective-permute-start.3 = (bf16[3,128,512]{2,1,0:T(8,128)(2,1)S(1)}, bf16[3,128,512]{2,1,0:T(8,128)(2,1)S(1)}, u32[]{:S(2)}, u32[]{:S(2)}) collective-permute-start(bf16[3,128,512]{2,1,0:T(8,128)(2,1)S(1)} %pad_maximum_fusion.refs_4_), channel_id=1, source_target_pairs={{0,8},{4,20},{8,0},{12,28},{16,24},{20,4},{24,16},{28,12},{1,9},{5... | collective-permute-start | bytes 1179656 | tf_op jit(solution)/shard_map/ppermute | solution.py:265
  18.7 17.4 %collective-permute-start.12 = (bf16[128,512]{1,0:T(8,128)(2,1)S(1)}, bf16[128,512]{1,0:T(8,128)(2,1)S(1)}, u32[]{:S(2)}, u32[]{:S(2)}) collective-permute-start(bf16[128,512]{1,0:T(8,128)(2,1)S(1)} %copy-done.2), channel_id=1, source_target_pairs={{0,24},{4,28},{8,16},{12,20},{16,8},{20,12},{24,0},{28,4},{1,25},{... | collective-permute-start | bytes 393224 | tf_op jit(solution)/shard_map/ppermute | solution.py:259
  20.2 16.0 %collective-permute-start.11 = (bf16[128,512]{1,0:T(8,128)(2,1)S(1)}, bf16[128,512]{1,0:T(8,128)(2,1)S(1)}, u32[]{:S(2)}, u32[]{:S(2)}) collective-permute-start(bf16[128,512]{1,0:T(8,128)(2,1)S(1)} %copy-done.2), channel_id=1, source_target_pairs={{0,16},{4,20},{8,24},{12,28},{16,0},{20,4},{24,8},{28,12},{1,17},{... | collective-permute-start | bytes 393224 | tf_op jit(solution)/shard_map/ppermute | solution.py:259
  20.7 13.9 %collective-permute-start.20 = (bf16[2,64,128]{2,1,0:T(8,128)(2,1)S(1)}, bf16[2,64,128]{2,1,0:T(8,128)(2,1)S(1)}, u32[]{:S(2)}, u32[]{:S(2)}) collective-permute-start(bf16[2,64,128]{2,1,0:T(8,128)(2,1)S(1)} %get-tuple-element.15), channel_id=1, source_target_pairs={{0,24},{4,28},{8,16},{12,20},{16,8},{20,12},{24,0},{28,4},{1,25},{... | collective-permute-start | bytes 98312 | tf_op jit(solution)/shard_map/ppermute | solution.py:259
  23.2 5.4 %collective-permute-start.18 = (bf16[2,64,128]{2,1,0:T(8,128)(2,1)S(1)}, bf16[2,64,128]{2,1,0:T(8,128)(2,1)S(1)}, u32[]{:S(2)}, u32[]{:S(2)}) collective-permute-start(bf16[2,64,128]{2,1,0:T(8,128)(2,1)S(1)} %get-tuple-element.17), channel_id=1, source_target_pairs={{0,8},{4,12},{8,0},{12,4},{16,24},{20,28},{24,16},{28,20},{1,9},{5... | collective-permute-start | bytes 98312 | tf_op jit(solution)/shard_map/ppermute | solution.py:259
  28.6 3.9 %collective-permute-start.19 = (bf16[2,64,128]{2,1,0:T(8,128)(2,1)S(1)}, bf16[2,64,128]{2,1,0:T(8,128)(2,1)S(1)}, u32[]{:S(2)}, u32[]{:S(2)}) collective-permute-start(bf16[2,64,128]{2,1,0:T(8,128)(2,1)S(1)} %get-tuple-element.18), channel_id=1, source_target_pairs={{0,16},{4,20},{8,24},{12,28},{16,0},{20,4},{24,8},{28,12},{1,17},{... | collective-permute-start | bytes 98312 | tf_op jit(solution)/shard_map/ppermute | solution.py:259
  32.5 18.5 %collective-permute-start.4 = (bf16[3,128,512]{2,1,0:T(8,128)(2,1)S(1)}, bf16[3,128,512]{2,1,0:T(8,128)(2,1)S(1)}, u32[]{:S(2)}, u32[]{:S(2)}) collective-permute-start(bf16[3,128,512]{2,1,0:T(8,128)(2,1)S(1)} %pad_maximum_fusion.refs_4_), channel_id=1, source_target_pairs={{0,16},{4,12},{8,24},{12,4},{16,0},{20,28},{24,8},{28,20},{1,17},{... | collective-permute-start | bytes 1179656 | tf_op jit(solution)/shard_map/ppermute | solution.py:265
  34.0 17.0 %collective-permute-start.5 = (bf16[3,128,512]{2,1,0:T(8,128)(2,1)S(1)}, bf16[3,128,512]{2,1,0:T(8,128)(2,1)S(1)}, u32[]{:S(2)}, u32[]{:S(2)}) collective-permute-start(bf16[3,128,512]{2,1,0:T(8,128)(2,1)S(1)} %collective-permute-done.3.refs_5_), channel_id=1, source_target_pairs={{0,16},{4,12},{8,24},{12,4},{16,0},{20,28},{24,8},{28,20},{1,17},{... | collective-permute-start | bytes 1179656 | tf_op jit(solution)/shard_map/ppermute | solution.py:265
  34.6 6.4 %collective-permute-start.10 = (bf16[128,512]{1,0:T(8,128)(2,1)S(1)}, bf16[128,512]{1,0:T(8,128)(2,1)S(1)}, u32[]{:S(2)}, u32[]{:S(2)}) collective-permute-start(bf16[128,512]{1,0:T(8,128)(2,1)S(1)} %copy-done.2), channel_id=1, source_target_pairs={{0,8},{4,12},{8,0},{12,4},{16,24},{20,28},{24,16},{28,20},{1,9},{5... | collective-permute-start | bytes 393224 | tf_op jit(solution)/shard_map/ppermute | solution.py:259
  36.1 4.9 %collective-permute-start.13 = (bf16[128,512]{1,0:T(8,128)(2,1)S(1)}, bf16[128,512]{1,0:T(8,128)(2,1)S(1)}, u32[]{:S(2)}, u32[]{:S(2)}) collective-permute-start(bf16[128,512]{1,0:T(8,128)(2,1)S(1)} %copy-done.2), channel_id=1, source_target_pairs={{0,4},{4,0},{8,12},{12,8},{16,20},{20,16},{24,28},{28,24},{1,5},{5... | collective-permute-start | bytes 393224 | tf_op jit(solution)/shard_map/ppermute | solution.py:259
  36.2 7.9 %collective-permute-start.23 = (bf16[528,128]{1,0:T(8,128)(2,1)S(1)}, bf16[528,128]{1,0:T(8,128)(2,1)S(1)}, u32[]{:S(2)}, u32[]{:S(2)}) collective-permute-start(bf16[528,128]{1,0:T(8,128)(2,1)S(1)} %constant_dynamic-update-slice_fusion.refs_20_), channel_id=1, source_target_pairs={{0,3},{1,2},{2,1},{3,0},{4,7},{5,6},{6,5},{7,4},{8,11},{9,10},{10,... | collective-permute-start | bytes 405512 | tf_op jit(solution)/shard_map/ppermute | solution.py:259
  41.0 9.1 %collective-permute-start.22 = (bf16[528,128]{1,0:T(8,128)(2,1)S(1)}, bf16[528,128]{1,0:T(8,128)(2,1)S(1)}, u32[]{:S(2)}, u32[]{:S(2)}) collective-permute-start(bf16[528,128]{1,0:T(8,128)(2,1)S(1)} %constant_dynamic-update-slice_fusion.refs_20_), channel_id=1, source_target_pairs={{0,2},{1,3},{2,0},{3,1},{4,6},{5,7},{6,4},{7,5},{8,10},{9,11},{10,... | collective-permute-start | bytes 405512 | tf_op jit(solution)/shard_map/ppermute | solution.py:259
  41.0 9.4 %collective-permute-start.21 = (bf16[528,128]{1,0:T(8,128)(2,1)S(1)}, bf16[528,128]{1,0:T(8,128)(2,1)S(1)}, u32[]{:S(2)}, u32[]{:S(2)}) collective-permute-start(bf16[528,128]{1,0:T(8,128)(2,1)S(1)} %constant_dynamic-update-slice_fusion.refs_20_), channel_id=1, source_target_pairs={{0,1},{1,0},{2,3},{3,2},{4,5},{5,4},{6,7},{7,6},{8,9},{9,8},{10,11... | collective-permute-start | bytes 405512 | tf_op jit(solution)/shard_map/ppermute | solution.py:259
  44.1 10.9 %collective-permute-start.6 = (bf16[3,128,512]{2,1,0:T(8,128)(2,1)S(1)}, bf16[3,128,512]{2,1,0:T(8,128)(2,1)S(1)}, u32[]{:S(2)}, u32[]{:S(2)}) collective-permute-start(bf16[3,128,512]{2,1,0:T(8,128)(2,1)S(1)} %pad_maximum_fusion.refs_4_), channel_id=1, source_target_pairs={{0,4},{4,0},{8,12},{12,8},{16,20},{20,16},{24,28},{28,24},{1,5},{5... | collective-permute-start | bytes 1179656 | tf_op jit(solution)/shard_map/ppermute | solution.py:259
  50.1 1.5 %collective-permute-start.16 = (bf16[128,512]{1,0:T(8,128)(2,1)S(1)}, bf16[128,512]{1,0:T(8,128)(2,1)S(1)}, u32[]{:S(2)}, u32[]{:S(2)}) collective-permute-start(bf16[128,512]{1,0:T(8,128)(2,1)S(1)} %collective-permute-done.12.refs_15_), channel_id=1, source_target_pairs={{0,4},{4,0},{8,12},{12,8},{16,20},{20,16},{24,28},{28,24},{1,5},{5... | collective-permute-start | bytes 393224 | tf_op jit(solution)/shard_map/ppermute | solution.py:259
  50.5 4.6 %collective-permute-start.7 = (bf16[3,128,512]{2,1,0:T(8,128)(2,1)S(1)}, bf16[3,128,512]{2,1,0:T(8,128)(2,1)S(1)}, u32[]{:S(2)}, u32[]{:S(2)}) collective-permute-start(bf16[3,128,512]{2,1,0:T(8,128)(2,1)S(1)} %collective-permute-done.3.refs_5_), channel_id=1, source_target_pairs={{0,4},{4,0},{8,12},{12,8},{16,20},{20,16},{24,28},{28,24},{1,5},{5... | collective-permute-start | bytes 1179656 | tf_op jit(solution)/shard_map/ppermute | solution.py:259
  51.0 4.0 %collective-permute-start.8 = (bf16[3,128,512]{2,1,0:T(8,128)(2,1)S(1)}, bf16[3,128,512]{2,1,0:T(8,128)(2,1)S(1)}, u32[]{:S(2)}, u32[]{:S(2)}) collective-permute-start(bf16[3,128,512]{2,1,0:T(8,128)(2,1)S(1)} %collective-permute-done.4.refs_6_), channel_id=1, source_target_pairs={{0,4},{4,0},{8,12},{12,8},{16,20},{20,16},{24,28},{28,24},{1,5},{5... | collective-permute-start | bytes 1179656 | tf_op jit(solution)/shard_map/ppermute | solution.py:259
  51.0 4.0 %collective-permute-start.9 = (bf16[3,128,512]{2,1,0:T(8,128)(2,1)S(1)}, bf16[3,128,512]{2,1,0:T(8,128)(2,1)S(1)}, u32[]{:S(2)}, u32[]{:S(2)}) collective-permute-start(bf16[3,128,512]{2,1,0:T(8,128)(2,1)S(1)} %collective-permute-done.5.refs_7_), channel_id=1, source_target_pairs={{0,4},{4,0},{8,12},{12,8},{16,20},{20,16},{24,28},{28,24},{1,5},{5... | collective-permute-start | bytes 1179656 | tf_op jit(solution)/shard_map/ppermute | solution.py:259
  51.5 2.1 %collective-permute-start.15 = (bf16[128,512]{1,0:T(8,128)(2,1)S(1)}, bf16[128,512]{1,0:T(8,128)(2,1)S(1)}, u32[]{:S(2)}, u32[]{:S(2)}) collective-permute-start(bf16[128,512]{1,0:T(8,128)(2,1)S(1)} %collective-permute-done.11.refs_14_), channel_id=1, source_target_pairs={{0,4},{4,0},{8,12},{12,8},{16,20},{20,16},{24,28},{28,24},{1,5},{5... | collective-permute-start | bytes 393224 | tf_op jit(solution)/shard_map/ppermute | solution.py:259
  53.7 1.4 %collective-permute-start.14 = (bf16[128,512]{1,0:T(8,128)(2,1)S(1)}, bf16[128,512]{1,0:T(8,128)(2,1)S(1)}, u32[]{:S(2)}, u32[]{:S(2)}) collective-permute-start(bf16[128,512]{1,0:T(8,128)(2,1)S(1)} %collective-permute-done.10.refs_13_), channel_id=1, source_target_pairs={{0,4},{4,0},{8,12},{12,8},{16,20},{20,16},{24,28},{28,24},{1,5},{5... | collective-permute-start | bytes 393224 | tf_op jit(solution)/shard_map/ppermute | solution.py:259
  (8 other events, 132.9 us)
